TPU v7x, 8 devices: a whole 2x2x1 slice. The times are simulated.
8 devices in a mesh: dp: 1 (over z), tp: 2 (over y), sp: 4 (over x, core).
Axes of the slice: x: 2, y: 2, z: 1, core: 2. Of those that a mesh axis runs over, the one named last changes fastest.
Arguments:
- hidden: bfloat16 [16, 3072], P('dp')
- positions: int32 [16], P('dp')
- norm_attn: float32 [3072], replicated
- norm_mlp: float32 [3072], replicated
- w_qkv: bfloat16 [3072, 9216], P(None, 'tp')
- w_out: bfloat16 [3072, 3072], P('tp')
- w_gate_up: bfloat16 [3072, 16384], P(None, 'tp')
- w_down: bfloat16 [8192, 3072], P('tp')
- k_cache: bfloat16 [16, 3072, 32, 96], P('dp', 'sp', 'tp')
- v_cache: bfloat16 [16, 3072, 32, 96], P('dp', 'sp', 'tp')
Outputs:
- output 1: bfloat16 [16, 3072], P('dp')
- output 2: bfloat16 [16, 3072, 32, 96], P('dp', 'sp', 'tp')
- output 3: bfloat16 [16, 3072, 32, 96], P('dp', 'sp', 'tp')
All inputs are finite; a program needn't handle non-finite values.
Results may differ from a plain program's by a relative error of at most 0.00882399.
Values sent between devices are 32-bit elements.
A program may use at most 1 GiB of HBM per device.

v0:
```python
import jax
import jax.numpy as jnp
from jax import lax
from jax.sharding import PartitionSpec as P

WINDOW = 2047
ROPE_BASE = 10000.0
NORM_EPS = 1e-5


def rms_norm(values, gain_vec):
    mean_sq = jnp.mean(values * values, axis=-1, keepdims=True)
    return values * lax.rsqrt(mean_sq + NORM_EPS) * gain_vec


def rope_tables(positions, head_dim):
    inv_freq = ROPE_BASE ** (-jnp.arange(0, head_dim, 2).astype(jnp.float32) / head_dim)
    angles = positions.astype(jnp.float32)[:, None] * inv_freq[None, :]
    angles = jnp.concatenate([angles, angles], axis=-1)
    return jnp.cos(angles), jnp.sin(angles)


def rotate_half(values, cos_tab, sin_tab):
    half_dim = values.shape[-1] // 2
    turned = jnp.concatenate([-values[..., half_dim:], values[..., :half_dim]], axis=-1)
    return values * cos_tab + turned * sin_tab


def new_entries(hidden, positions, norm_attn, w_qkv, kv_count, head_dim):
    num_rows = hidden.shape[0]
    resid_in = hidden.astype(jnp.float32)
    normed = rms_norm(resid_in, norm_attn).astype(jnp.bfloat16)
    group_size = w_qkv.shape[1] // (kv_count * head_dim) - 2
    qkv_proj = jnp.dot(normed, w_qkv, preferred_element_type=jnp.float32).reshape(num_rows, kv_count, group_size + 2, head_dim)
    cos_tab, sin_tab = rope_tables(positions, head_dim)
    q_new = rotate_half(qkv_proj[:, :, :group_size], cos_tab[:, None, None], sin_tab[:, None, None]).astype(jnp.bfloat16)
    k_new = rotate_half(qkv_proj[:, :, group_size], cos_tab[:, None], sin_tab[:, None]).astype(jnp.bfloat16)
    v_new = qkv_proj[:, :, group_size + 1].astype(jnp.bfloat16)
    return resid_in, q_new, k_new, v_new


def write_entry(cache, entry, slot_ids, positions):
    at_slot = (slot_ids[None, :] == positions[:, None])[:, :, None, None]
    return jnp.where(at_slot, entry[:, None], cache)


def window_attention(q_new, k_block, v_block, slot_ids, positions):
    score_scale = q_new.shape[-1] ** -0.5
    scores = jnp.einsum('bkgd,bjkd->bkgj', q_new, k_block, preferred_element_type=jnp.float32) * score_scale
    in_window = (slot_ids[None, :] <= positions[:, None]) & (slot_ids[None, :] >= positions[:, None] - WINDOW)
    scores = jnp.where(in_window[:, None, None, :], scores, -jnp.inf)
    glob_max = lax.pmax(jnp.max(scores, axis=-1), 'sp')
    weights = jnp.exp(scores - glob_max[..., None])
    weight_sum = lax.psum(jnp.sum(weights, axis=-1), 'sp')
    acc_sum = lax.psum(jnp.einsum('bkgj,bjkd->bkgd', weights.astype(jnp.bfloat16), v_block, preferred_element_type=jnp.float32), 'sp')
    return (acc_sum / weight_sum[..., None]).astype(jnp.bfloat16)


def layer_tail(resid_in, attended, norm_mlp, w_out, w_gate_up, w_down):
    out_part = jnp.dot(attended, w_out, preferred_element_type=jnp.float32).astype(jnp.bfloat16).astype(jnp.float32)
    mid_resid = resid_in + lax.psum(out_part, 'tp')
    normed_mlp = rms_norm(mid_resid, norm_mlp).astype(jnp.bfloat16)
    gate_up = jnp.dot(normed_mlp, w_gate_up, preferred_element_type=jnp.float32)
    ffn_local = w_down.shape[0]
    act_vals = (jax.nn.silu(gate_up[:, :ffn_local]) * gate_up[:, ffn_local:]).astype(jnp.bfloat16)
    down_part = jnp.dot(act_vals, w_down, preferred_element_type=jnp.float32).astype(jnp.bfloat16).astype(jnp.float32)
    result = mid_resid + lax.psum(down_part, 'tp')
    return result.astype(jnp.bfloat16)


def solution(mesh):
    cache_spec = P('dp', 'sp', 'tp', None)

    def local_step(hidden, positions, norm_attn, norm_mlp, w_qkv, w_out, w_gate_up, w_down, k_cache, v_cache):
        num_rows, block_len, kv_local, head_dim = k_cache.shape
        resid_in, q_new, k_new, v_new = new_entries(hidden, positions, norm_attn, w_qkv, kv_local, head_dim)
        slot_ids = lax.axis_index('sp') * block_len + jnp.arange(block_len)
        k_upd = write_entry(k_cache, k_new, slot_ids, positions)
        v_upd = write_entry(v_cache, v_new, slot_ids, positions)
        attended = window_attention(q_new, k_upd, v_upd, slot_ids, positions).reshape(num_rows, -1)
        result = layer_tail(resid_in, attended, norm_mlp, w_out, w_gate_up, w_down)
        return result, k_upd, v_upd

    return jax.shard_map(local_step, mesh=mesh, in_specs=(P('dp', None), P('dp'), P(None), P(None), P(None, 'tp'), P('tp', None), P(None, 'tp'), P('tp', None), cache_spec, cache_spec), out_specs=(P('dp', None), cache_spec, cache_spec), check_vma=False)
```

profile of v0, /device:TPU:0, one launch (start us, length us, event | category | flops | bytes accessed | tf_op | source)
XLA Modules:
  0.0 218.9 jit_solution(7329235655281395221)
XLA Ops:
  7.2 0.0 copy-start.3
  7.2 0.0 all-reduce.4.cloned.1.call-start
  7.2 1.0 fusion.10
  8.3 11.1 %fusion.23 = f32[16,4608]{1,0:T(8,128)S(1)} fusion(bf16[3072,4608]{1,0:T(8,128)(2,1)} %param.14, bf16[16,3072]{1,0:T(8,128)(2,1)} %param.10, f32[3072]{0:T(1024)} %param.12, f32[16]{0:T(128)S(1)} %add_rsqrt_fusion.1), kind=kOutput, calls=%fused_computation.41 | convolution fusion | flops 453181440 | bytes 28717120 | tf_op jit(solution)/shard_map/dot_general | solution.py:34
  19.4 0.4 reshape.299
  19.8 0.1 slice.42
  19.9 0.1 slice.63
  20.1 0.4 slice_negate_fusion.1
  20.5 0.0 copy-done.3
  20.5 0.1 broadcast_multiply_fusion
  20.6 0.1 fusion.32
  20.7 0.1 slice_negate_fusion
  20.8 0.1 compare_and_fusion
  20.9 0.1 fusion.16
  21.0 49.3 %broadcast_select_fusion.1 = (bf16[16,768,16,96]{1,3,2,0:T(8,128)(2,1)}, bf16[16,768,16,96]{1,3,2,0:T(8,128)(2,1)}) fusion(bf16[16,768,16,96]{1,3,2,0:T(8,128)(2,1)} %param.18, pred[16,768]{1,0:T(8,128)(4,1)S(1)} %get-tuple-element.14, bf16[16,16,96]{2,1,0:T(8,128)(2,1)S(1)} %fusion.16, bf16[16,768,16,96]{1,3,2,0:T(8,128)(2,1)} %param.19, ...), kind=kLoop, calls=%fused_computation.1 | loop fusion | flops 37748736 | bytes 151105536 | tf_op jit(solution)/shard_map/jit(_where)/select_n | solution.py:44
  70.3 13.9 %fusion.17 = f32[16,16,1,768]{3,2,1,0:T(1,128)S(1)} fusion(bf16[16,768,16,96]{1,3,2,0:T(8,128)(2,1)} %get-tuple-element.9, f32[16,16,3,96]{3,2,1,0:T(4,128)S(1)} %reshape.299, f32[16,16,1,48]{3,2,1,0:T(1,128)S(1)} %get-tuple-element.6, f32[16,16,1,48]{3,2,1,0:T(1,128)S(1)} %get-tuple-element.5, f32[16,96]{1,0:T(8,128)S(1)} %get-tuple-element.12, ...), kind=kOutput, calls=%fused_computation.35 | convolution fusion | flops 37871616 | bytes 38944768 | tf_op jit(solution)/shard_map/bkgd,bjkd->bkgj/dot_general | solution.py:49
  84.2 0.0 copy-start
  84.2 0.0 copy-start.2
  84.3 0.2 fusion.7
  84.4 8.9 %pmax.7 = f32[16,16]{1,0:T(8,128)S(1)} all-reduce(f32[16,16]{1,0:T(8,128)S(1)} %fusion.7), channel_id=1, replica_groups=mesh['dp'=1,'tp'=2,'sp'=4] {'sp'}, use_global_device_ids=true, to_apply=%region_2.3 | all-reduce | flops 256 | bytes 2048 | tf_op jit(solution)/shard_map/pmax | solution.py:52
  93.4 0.3 fusion.5
  93.7 16.6 %fusion.3 = f32[16,16,1,96]{3,2,1,0:T(1,128)} fusion(bf16[16,768,16,96]{1,3,2,0:T(8,128)(2,1)} %get-tuple-element.10, bf16[16,16,768,1]{2,1,0,3:T(8,128)(2,1)S(1)} %get-tuple-element.4), kind=kOutput, calls=%fused_computation.8 | convolution fusion | flops 37748736 | bytes 38240256 | tf_op jit(solution)/shard_map/bkgj,bjkd->bkgd/dot_general | solution.py:55
  110.3 0.0 all-reduce.4.cloned.1.call-update
  110.4 0.0 all-reduce.6.cloned.1.call-start
  110.4 5.9 %psum.29 = f32[16,16]{1,0:T(8,128)S(1)} all-reduce(f32[16,16]{1,0:T(8,128)S(1)} %get-tuple-element.3), channel_id=1, replica_groups=mesh['dp'=1,'tp'=2,'sp'=4] {'sp'}, use_global_device_ids=true, to_apply=%region_5.6 | all-reduce | flops 256 | bytes 2048 | tf_op jit(solution)/shard_map/psum | solution.py:54
  116.3 20.4 %all-reduce.4.cloned.1.call-done = f32[16,16,1,96]{3,1,0,2:T(8,128)} async-done(((f32[16,16,1,96]{3,1,0,2:T(8,128)}), f32[16,16,1,96]{3,1,0,2:T(8,128)}) %all-reduce.4.cloned.1.call-update) | async-done | bytes 98320 | tf_op jit(solution)/shard_map/psum | solution.py:55
  136.7 1.0 divide_convert_fusion
  137.7 0.1 reshape.301
  137.9 5.7 %fusion.1 = f32[16,3072]{1,0:T(8,128)} fusion(bf16[16,1536]{1,0:T(8,128)(2,1)S(1)} %reshape.301, bf16[1536,3072]{1,0:T(8,128)(2,1)} %param.15), kind=kOutput, calls=%fused_computation.5 | convolution fusion | flops 151093248 | bytes 9682944 | tf_op jit(solution)/shard_map/dot_general | solution.py:60
  143.6 0.0 all-reduce.6.cloned.1.call-update
  143.6 0.2 all-reduce.8.cloned.1.call-start
  143.8 16.6 %all-reduce.6.cloned.1.call-done = f32[16,3072]{1,0:T(8,128)} async-done(((f32[16,3072]{1,0:T(8,128)}), f32[16,3072]{1,0:T(8,128)}) %all-reduce.6.cloned.1.call-update) | async-done | bytes 196624 | tf_op jit(solution)/shard_map/psum | solution.py:61
  160.4 0.0 copy-done
  160.4 1.1 multiply_reduce_fusion
  161.4 0.0 copy-done.2
  161.5 0.0 copy-start.1
  161.5 21.9 %fusion.22 = f32[16,8192]{1,0:T(8,128)S(1)} fusion(bf16[3072,8192]{1,0:T(8,128)(2,1)} %param.16, f32[3072]{0:T(1024)S(1)} %copy-done.2, f32[16]{0:T(128)S(1)} %add_rsqrt_fusion, f32[16,3072]{1,0:T(8,128)} %all-reduce.6.cloned.1.call-done, bf16[16,3072]{1,0:T(8,128)(2,1)S(1)} %copy-done), kind=kOutput, calls=%fused_computation.40 | convolution fusion | flops 805552128 | bytes 51163200 | tf_op jit(solution)/shard_map/dot_general | solution.py:63
  183.3 10.6 %fusion = f32[16,3072]{1,0:T(8,128)} fusion(bf16[4096,3072]{1,0:T(8,128)(2,1)} %param.17, f32[16,8192]{1,0:T(8,128)S(1)} %fusion.22), kind=kOutput, calls=%fused_computation.3 | convolution fusion | flops 403144704 | bytes 25886720 | tf_op jit(solution)/shard_map/dot_general | solution.py:66
  193.9 0.0 all-reduce.8.cloned.1.call-update
  193.9 16.8 %all-reduce.8.cloned.1.call-done = f32[16,3072]{1,0:T(8,128)} async-done(((f32[16,3072]{1,0:T(8,128)}), f32[16,3072]{1,0:T(8,128)}) %all-reduce.8.cloned.1.call-update) | async-done | bytes 196624 | tf_op jit(solution)/shard_map/psum | solution.py:67
  210.7 0.0 copy-done.1
  210.7 1.6 add_convert_fusion
  (6 shorter events, 0.0 us)
Async XLA Ops:
  7.2 13.3 %copy-start.3 = (s32[16]{0:T(128)S(1)}, s32[16]{0:T(128)}, u32[]{:S(2)}) copy-start(s32[16]{0:T(128)} %param.11) | copy-start | bytes 196
  7.2 129.5 %all-reduce.4.cloned.1.call-start = ((), (), s32[]{:S(2)}) async-start(), calls=%async_computation | async-start | bytes 262144 | tf_op jit(solution)/shard_map/psum | solution.py:55
  84.2 76.1 %copy-start = (bf16[16,3072]{1,0:T(8,128)(2,1)S(1)}, bf16[16,3072]{1,0:T(8,128)(2,1)}, u32[]{:S(2)}) copy-start(bf16[16,3072]{1,0:T(8,128)(2,1)} %param.10) | copy-start | bytes 294916
  84.2 77.2 %copy-start.2 = (f32[3072]{0:T(1024)S(1)}, f32[3072]{0:T(1024)}, u32[]{:S(2)}) copy-start(f32[3072]{0:T(1024)} %param.13) | copy-start | bytes 36868
  110.4 50.0 %all-reduce.6.cloned.1.call-start = ((), (), s32[]{:S(2)}) async-start(), calls=%async_computation.1 | async-start | bytes 393216 | tf_op jit(solution)/shard_map/psum | solution.py:61
  143.6 67.2 %all-reduce.8.cloned.1.call-start = ((), (), s32[]{:S(2)}) async-start(), calls=%async_computation.2 | async-start | bytes 393216 | tf_op jit(solution)/shard_map/psum | solution.py:67
  161.5 49.3 %copy-start.1 = (f32[16,3072]{1,0:T(8,128)S(1)}, f32[16,3072]{1,0:T(8,128)}, u32[]{:S(2)}) copy-start(f32[16,3072]{1,0:T(8,128)} %all-reduce.6.cloned.1.call-done) | copy-start | bytes 589828
Sparse Core Ops, SparseCore 0:
  110.5 26.1 all-reduce.3
  143.7 16.6 all-reduce.5
  194.1 16.6 all-reduce.7
where the time goes:
time: 219 us
  matrix products  79.8 us (36%)
  other arithmetic  55.4 us (25%)
  waiting for transfers between devices  53.8 us (25%)
  blocking collectives  14.8 us (7%)
  between operations  13.9 us (6%)
    select_n x1, other arithmetic, write_entry(): return jnp.where(at_slot, entry[:, None], cache)  49.3 us
    dot_general x1, matrix products, layer_tail(): gate_up = jnp.dot(normed_mlp, w_gate_up, preferred_element_type=jnp.float32)  21.9 us
    psum x1, waiting for transfers between devices, window_attention(): lax.psum(jnp.einsum('bkgj,bjkd->bkgd', weights.astype(jnp.bfloat16), v_bl...  20.4 us
    psum x1, waiting for transfers between devices, layer_tail(): result = mid_resid + lax.psum(down_part, 'tp')  16.8 us
    dot_general x1, matrix products, window_attention(): jnp.einsum('bkgj,bjkd->bkgd', weights.astype(jnp.bfloat16), v_block, pref...  16.6 us
    psum x1, waiting for transfers between devices, layer_tail(): mid_resid = resid_in + lax.psum(out_part, 'tp')  16.6 us
    dot_general x1, matrix products, window_attention(): jnp.einsum('bkgd,bjkd->bkgj', q_new, k_block, preferred_element_type=jnp....  13.9 us
    dot_general x1, matrix products, new_entries(): jnp.dot(normed, w_qkv, preferred_element_type=jnp.float32)  11.1 us
  transfers between devices with their start and end apart: 3, of which 3 were waited for; matrix products, arithmetic and copies ran while one was open for 0% of the time, Pallas kernels for 0%

commit v1 on v0

v1 whole, which is shorter than its diff:
```python
import functools

import jax
import jax.numpy as jnp
from jax import lax
from jax.experimental import pallas as pl
from jax.experimental.pallas import tpu as pltpu
from jax.sharding import PartitionSpec as P

WINDOW = 2047
ROPE_BASE = 10000.0
NORM_EPS = 1e-5
NEG = -1e30
MESH = pl.DeviceIdType.MESH


def rms_norm(values, gain_vec):
    mean_sq = jnp.mean(values * values, axis=-1, keepdims=True)
    return values * lax.rsqrt(mean_sq + NORM_EPS) * gain_vec


def rope_tables(positions, head_dim):
    inv_freq = ROPE_BASE ** (-jnp.arange(0, head_dim, 2).astype(jnp.float32) / head_dim)
    angles = positions.astype(jnp.float32)[:, None] * inv_freq[None, :]
    angles = jnp.concatenate([angles, angles], axis=-1)
    return jnp.cos(angles), jnp.sin(angles)


def rotate_half(values, cos_tab, sin_tab):
    half_dim = values.shape[-1] // 2
    turned = jnp.concatenate([-values[..., half_dim:], values[..., :half_dim]], axis=-1)
    return values * cos_tab + turned * sin_tab


def new_entries(hidden, positions, norm_attn, w_qkv, kv_count, head_dim):
    num_rows = hidden.shape[0]
    resid_in = hidden.astype(jnp.float32)
    normed = rms_norm(resid_in, norm_attn).astype(jnp.bfloat16)
    qkv_proj = jnp.dot(normed, w_qkv, preferred_element_type=jnp.float32).reshape(num_rows, kv_count, 3, head_dim)
    cos_tab, sin_tab = rope_tables(positions, head_dim)
    q_new = rotate_half(qkv_proj[:, :, 0], cos_tab[:, None], sin_tab[:, None])
    k_new = rotate_half(qkv_proj[:, :, 1], cos_tab[:, None], sin_tab[:, None])
    v_new = qkv_proj[:, :, 2]
    rows = lambda x: x.reshape(num_rows, -1)
    return rows(q_new), rows(k_new), rows(v_new)


def attend_kernel(pos_ref, q_ref, kn_ref, vn_ref, k_ref, v_ref, ko_ref, vo_ref, o_ref, ml_ref, kt_ref, vt_ref):
    b = pl.program_id(0)
    rows, heads, dim, block = q_ref.shape[0], k_ref.shape[1], k_ref.shape[2], k_ref.shape[3]
    width = heads * dim

    @pl.when(b == 0)
    def _():
        pad = jnp.zeros((128 - rows, width), jnp.float32)
        kt_ref[...] = jnp.concatenate([kn_ref[...], pad], axis=0).T
        vt_ref[...] = jnp.concatenate([vn_ref[...], pad], axis=0).T

    base = lax.axis_index('sp') * block
    pos = pos_ref[b]
    slot = pos - base
    ko_ref[...] = k_ref[...]
    vo_ref[...] = v_ref[...]

    @pl.when((slot >= 0) & (slot < block))
    def _():
        lane = lax.rem(slot, 128)
        start = pl.multiple_of(slot - lane, 128)
        shift = lax.rem(lane - b + 128, 128)
        hit = lax.broadcasted_iota(jnp.int32, (width, 128), 1) == lane
        for new_ref, out_ref in ((kt_ref, ko_ref), (vt_ref, vo_ref)):
            entry = pltpu.roll(new_ref[...], shift, 1)
            old = out_ref[0, :, :, pl.ds(start, 128)].reshape(width, 128).astype(jnp.float32)
            out_ref[0, :, :, pl.ds(start, 128)] = jnp.where(hit, entry, old).astype(jnp.bfloat16).reshape(heads, dim, 128)

    own = lax.broadcasted_iota(jnp.int32, (heads, width), 1) // dim == lax.broadcasted_iota(jnp.int32, (heads, width), 0)
    q_row = jnp.broadcast_to(q_ref[pl.ds(b, 1), :], (heads, width))
    q_diag = jnp.where(own, q_row, 0.0).astype(jnp.bfloat16)
    scores = jnp.dot(q_diag, ko_ref[0].reshape(width, block), preferred_element_type=jnp.float32) * (dim ** -0.5)
    slot_ids = lax.broadcasted_iota(jnp.int32, (heads, block), 1) + base
    in_window = (slot_ids <= pos) & (slot_ids >= pos - WINDOW)
    scores = jnp.where(in_window, scores, NEG)
    row_max = jnp.max(scores, axis=1, keepdims=True)
    weights = jnp.where(in_window, jnp.exp(scores - row_max), 0.0)
    row_sum = jnp.sum(weights, axis=1, keepdims=True)
    acc = lax.dot_general(weights.astype(jnp.bfloat16), vo_ref[0].reshape(width, block), (((1,), (1,)), ((), ())), preferred_element_type=jnp.float32)
    o_ref[pl.ds(b, 1), :] = jnp.sum(jnp.where(own, acc, 0.0), axis=0, keepdims=True)
    lane_ids = lax.broadcasted_iota(jnp.int32, (heads, 128), 1)
    head_ids = lax.broadcasted_iota(jnp.int32, (heads, 128), 0)
    stats = jnp.where(lane_ids == head_ids, row_max, 0.0) + jnp.where(lane_ids == head_ids + heads, row_sum, 0.0)
    ml_ref[pl.ds(b, 1), :] = jnp.sum(stats, axis=0, keepdims=True)


def attend(positions, q_rows, k_rows, v_rows, k_t, v_t):
    rows, heads, dim, block = k_t.shape
    width = heads * dim
    full = lambda shape: pl.BlockSpec(shape, lambda b, pos: (0, 0))
    cache = pl.BlockSpec((1, heads, dim, block), lambda b, pos: (b, 0, 0, 0))
    return pl.pallas_call(
        attend_kernel,
        out_shape=(jax.ShapeDtypeStruct(k_t.shape, k_t.dtype), jax.ShapeDtypeStruct(v_t.shape, v_t.dtype), jax.ShapeDtypeStruct((rows, width), jnp.float32), jax.ShapeDtypeStruct((rows, 128), jnp.float32)),
        grid_spec=pltpu.PrefetchScalarGridSpec(
            num_scalar_prefetch=1,
            grid=(rows,),
            in_specs=[full((rows, width))] * 3 + [cache] * 2,
            out_specs=(cache, cache, full((rows, width)), full((rows, 128))),
            scratch_shapes=[pltpu.VMEM((width, 128), jnp.float32)] * 2,
        ),
        compiler_params=pltpu.CompilerParams(dimension_semantics=("arbitrary",), vmem_limit_bytes=48 << 20),
        name="attend",
    )(positions, q_rows, k_rows, v_rows, k_t, v_t)


def layer_tail(resid_in, attended, norm_mlp, w_out, w_gate_up, w_down):
    out_part = jnp.dot(attended, w_out, preferred_element_type=jnp.float32).astype(jnp.bfloat16).astype(jnp.float32)
    mid_resid = resid_in + lax.psum(out_part, 'tp')
    normed_mlp = rms_norm(mid_resid, norm_mlp).astype(jnp.bfloat16)
    gate_up = jnp.dot(normed_mlp, w_gate_up, preferred_element_type=jnp.float32)
    ffn_local = w_down.shape[0]
    act_vals = (jax.nn.silu(gate_up[:, :ffn_local]) * gate_up[:, ffn_local:]).astype(jnp.bfloat16)
    down_part = jnp.dot(act_vals, w_down, preferred_element_type=jnp.float32).astype(jnp.bfloat16).astype(jnp.float32)
    result = mid_resid + lax.psum(down_part, 'tp')
    return result.astype(jnp.bfloat16)


def solution(mesh):
    cache_spec = P('dp', 'sp', 'tp', None)

    def local_step(hidden, positions, norm_attn, norm_mlp, w_qkv, w_out, w_gate_up, w_down, k_cache, v_cache):
        num_rows, block_len, kv_local, head_dim = k_cache.shape
        q_rows, k_rows, v_rows = new_entries(hidden, positions, norm_attn, w_qkv, kv_local, head_dim)
        k_upd, v_upd, o_part, stats = attend(positions, q_rows, k_rows, v_rows, k_cache.transpose(0, 2, 3, 1), v_cache.transpose(0, 2, 3, 1))
        row_max, row_sum = stats[:, :kv_local], stats[:, kv_local:2 * kv_local]
        alpha = jnp.exp(row_max - lax.pmax(row_max, 'sp'))
        total = lax.psum(alpha * row_sum, 'sp')
        acc = lax.psum(o_part.reshape(num_rows, kv_local, head_dim) * alpha[..., None], 'sp')
        attended = (acc / total[..., None]).astype(jnp.bfloat16).reshape(num_rows, -1)
        result = layer_tail(hidden.astype(jnp.float32), attended, norm_mlp, w_out, w_gate_up, w_down)
        return result, k_upd.transpose(0, 3, 1, 2), v_upd.transpose(0, 3, 1, 2)

    return jax.shard_map(local_step, mesh=mesh, in_specs=(P('dp', None), P('dp'), P(None), P(None), P(None, 'tp'), P('tp', None), P(None, 'tp'), P('tp', None), cache_spec, cache_spec), out_specs=(P('dp', None), cache_spec, cache_spec), check_vma=False)
```

time: 219 us -> 191 us (0.87)
  Pallas kernels: 0 us -> 51.7 us
  other arithmetic: 55.4 us -> 6.73 us
  matrix products: 79.8 us -> 46.2 us
    pallas_call x0 -> x1, Pallas kernels: none -> 51.7 us  [attend(): pl.pallas_call(attend_kernel, out_shape=(jax.ShapeDtypeStruct(k_t.shape,...]
    select_n x1 -> x0, other arithmetic: 49.3 us -> none  [write_entry(): return jnp.where(at_slot, entry[:, None], cache)]
    dot_general x2 -> x0, matrix products: 30.5 us -> none  [the longest x1 16.6 us: window_attention(): jnp.einsum('bkgj,bjkd->bkgd', weights.astype(jnp.bfloat16), v_block, pref...]
    dot_general x1, matrix products: 21.9 us -> 18.8 us  [layer_tail(): gate_up = jnp.dot(normed_mlp, w_gate_up, preferred_element_type=jnp.float32)]
where the time goes in v1:
time: 191 us
  waiting for transfers between devices  53.8 us (28%)
  Pallas kernels  51.7 us (27%)
  matrix products  46.2 us (24%)
  blocking collectives  15.7 us (8%)
  between operations  13.9 us (7%)
  other arithmetic  6.73 us (4%)
  local copies, waits for them, and re-layouts  2.21 us (1%)
    pallas_call x1, Pallas kernels, attend(): pl.pallas_call(attend_kernel, out_shape=(jax.ShapeDtypeStruct(k_t.shape,...  51.7 us
    psum x1, waiting for transfers between devices, local_step(): lax.psum(o_part.reshape(num_rows, kv_local, head_dim) * alpha[..., None],...  20.4 us
    dot_general x1, matrix products, layer_tail(): gate_up = jnp.dot(normed_mlp, w_gate_up, preferred_element_type=jnp.float32)  18.8 us
    psum x1, waiting for transfers between devices, layer_tail(): result = mid_resid + lax.psum(down_part, 'tp')  16.8 us
    psum x1, waiting for transfers between devices, layer_tail(): mid_resid = resid_in + lax.psum(out_part, 'tp')  16.6 us
    dot_general x1, matrix products, new_entries(): jnp.dot(normed, w_qkv, preferred_element_type=jnp.float32)  11.1 us
    dot_general x1, matrix products, layer_tail(): jnp.dot(act_vals, w_down, preferred_element_type=jnp.float32)  10.6 us
    pmax x1, blocking collectives, local_step(): alpha = jnp.exp(row_max - lax.pmax(row_max, 'sp'))  9.83 us
  transfers between devices with their start and end apart: 3, of which 3 were waited for; matrix products, arithmetic and copies ran while one was open for 0% of the time, Pallas kernels for 0%

profile of v1, /device:TPU:0, one launch (start us, length us, event | category | flops | bytes accessed | tf_op | source)
XLA Modules:
  0.0 190.5 jit_solution(14632096601287093756)
XLA Ops:
  7.2 0.0 copy-start
  7.2 0.0 all-reduce.4.cloned.1.call-start
  7.2 0.7 convert_element_type.43
  7.9 1.0 fusion.3
  8.9 0.1 broadcast_multiply_fusion.1
  9.0 0.1 fusion.16
  9.2 0.1 mul.135
  9.3 11.1 %fusion.9 = f32[16,4608]{1,0:T(8,128)S(1)} fusion(bf16[3072,4608]{1,0:T(8,128)(2,1)} %param.14, bf16[16,3072]{1,0:T(8,128)(2,1)} %param.10, f32[3072]{0:T(1024)} %param.12, f32[16]{0:T(128)S(1)} %add_rsqrt_fusion.1), kind=kOutput, calls=%fused_computation.23 | convolution fusion | flops 453181440 | bytes 28717120 | tf_op jit(solution)/shard_map/dot_general | solution.py:39
  20.4 0.4 reshape.106
  20.8 0.9 slice_reduce_fusion
  21.7 0.1 reshape_squeeze.3.vn_ref
  21.8 0.1 squeeze.12
  21.9 0.1 squeeze.10
  22.0 0.1 slice_negate_fusion
  22.2 0.1 maximum_multiply_fusion.1
  22.3 0.1 mul.142
  22.4 0.1 mul.139
  22.5 0.0 copy-done
  22.6 0.0 copy-start.1
  22.6 0.0 copy-start.3
  22.6 51.7 %attend.1 = (bf16[16,16,96,768]{3,2,1,0:T(8,128)(2,1)}, bf16[16,16,96,768]{3,2,1,0:T(8,128)(2,1)}, f32[16,1536]{1,0:T(8,128)S(1)}, f32[16,128]{1,0:T(8,128)S(1)}) custom-call(s32[16]{0:T(128)S(1)} %copy-done, f32[16,1536]{1,0:T(8,128)S(1)} %get-tuple-element.22.q_ref, f32[16,1536]{1,0:T(8,128)S(1)} %get-tuple-element.21.kn_ref, ...), custom_call_target="tpu_custom_call" | custom-call | tf_op jit(solution)/shard_map/attend/pallas_call | solution.py:99
  74.2 9.8 %pmax.7 = f32[16,16]{1,0:T(8,128)S(1)} all-reduce(f32[16,16]{1,0:T(8,128)S(1)} %bitcast.18), channel_id=1, replica_groups=mesh['dp'=1,'tp'=2,'sp'=4] {'sp'}, use_global_device_ids=true, to_apply=%region_1.0 | all-reduce | flops 256 | bytes 2048 | tf_op jit(solution)/shard_map/pmax | solution.py:134
  84.1 0.1 slice_multiply_fusion.1
  84.2 0.1 reshape.107
  84.3 0.8 broadcast_multiply_fusion
  85.0 0.0 all-reduce.4.cloned.1.call-update
  85.0 0.0 all-reduce.6.cloned.1.call-start
  85.1 5.9 %psum.29 = f32[16,16]{1,0:T(8,128)S(1)} all-reduce(f32[16,16]{1,0:T(8,128)S(1)} %get-tuple-element.13), channel_id=1, replica_groups=mesh['dp'=1,'tp'=2,'sp'=4] {'sp'}, use_global_device_ids=true, to_apply=%region_3.0 | all-reduce | flops 256 | bytes 2048 | tf_op jit(solution)/shard_map/psum | solution.py:135
  91.0 20.4 %all-reduce.4.cloned.1.call-done = f32[16,16,96]{2,1,0:T(8,128)} async-done(((f32[16,16,96]{2,1,0:T(8,128)}), f32[16,16,96]{2,1,0:T(8,128)}) %all-reduce.4.cloned.1.call-update) | async-done | bytes 98320 | tf_op jit(solution)/shard_map/psum | solution.py:136
  111.4 1.0 divide_convert_fusion
  112.4 0.1 reshape.108
  112.6 5.7 %fusion.1 = f32[16,3072]{1,0:T(8,128)} fusion(bf16[16,1536]{1,0:T(8,128)(2,1)S(1)} %reshape.108, bf16[1536,3072]{1,0:T(8,128)(2,1)} %param.15), kind=kOutput, calls=%fused_computation.3 | convolution fusion | flops 151093248 | bytes 9682944 | tf_op jit(solution)/shard_map/dot_general | solution.py:115
  118.3 0.0 all-reduce.6.cloned.1.call-update
  118.3 0.2 all-reduce.8.cloned.1.call-start
  118.5 16.6 %all-reduce.6.cloned.1.call-done = f32[16,3072]{1,0:T(8,128)} async-done(((f32[16,3072]{1,0:T(8,128)}), f32[16,3072]{1,0:T(8,128)}) %all-reduce.6.cloned.1.call-update) | async-done | bytes 196624 | tf_op jit(solution)/shard_map/psum | solution.py:116
  135.1 0.0 copy-done.1
  135.1 1.1 multiply_reduce_fusion
  136.2 0.0 copy-done.3
  136.2 18.8 %fusion.8 = f32[16,8192]{1,0:T(8,128)S(1)} fusion(bf16[3072,8192]{1,0:T(8,128)(2,1)} %param.16, f32[3072]{0:T(1024)S(1)} %copy-done.3, f32[16]{0:T(128)S(1)} %add_rsqrt_fusion, f32[16,3072]{1,0:T(8,128)} %all-reduce.6.cloned.1.call-done, bf16[16,3072]{1,0:T(8,128)(2,1)S(1)} %copy-done.1), kind=kOutput, calls=%fused_computation.22 | convolution fusion | flops 805552128 | bytes 51163200 | tf_op jit(solution)/shard_map/dot_general | solution.py:118
  155.0 0.0 copy-start.2
  155.0 10.6 %fusion = f32[16,3072]{1,0:T(8,128)} fusion(bf16[4096,3072]{1,0:T(8,128)(2,1)} %param.17, f32[16,8192]{1,0:T(8,128)S(1)} %fusion.8), kind=kOutput, calls=%fused_computation.1 | convolution fusion | flops 403144704 | bytes 25886720 | tf_op jit(solution)/shard_map/dot_general | solution.py:121
  165.6 0.0 all-reduce.8.cloned.1.call-update
  165.6 16.8 %all-reduce.8.cloned.1.call-done = f32[16,3072]{1,0:T(8,128)} async-done(((f32[16,3072]{1,0:T(8,128)}), f32[16,3072]{1,0:T(8,128)}) %all-reduce.8.cloned.1.call-update) | async-done | bytes 196624 | tf_op jit(solution)/shard_map/psum | solution.py:122
  182.4 0.0 copy-done.2
  182.4 1.6 add_convert_fusion
  (5 shorter events, 0.1 us)
Async XLA Ops:
  7.2 15.4 %copy-start = (s32[16]{0:T(128)S(1)}, s32[16]{0:T(128)}, u32[]{:S(2)}) copy-start(s32[16]{0:T(128)} %pos_ref.1) | copy-start | bytes 196
  7.2 104.2 %all-reduce.4.cloned.1.call-start = ((), (), s32[]{:S(2)}) async-start(), calls=%async_computation | async-start | bytes 262144 | tf_op jit(solution)/shard_map/psum | solution.py:136
  22.6 112.5 %copy-start.1 = (bf16[16,3072]{1,0:T(8,128)(2,1)S(1)}, bf16[16,3072]{1,0:T(8,128)(2,1)}, u32[]{:S(2)}) copy-start(bf16[16,3072]{1,0:T(8,128)(2,1)} %param.10) | copy-start | bytes 294916
  22.6 113.6 %copy-start.3 = (f32[3072]{0:T(1024)S(1)}, f32[3072]{0:T(1024)}, u32[]{:S(2)}) copy-start(f32[3072]{0:T(1024)} %param.13) | copy-start | bytes 36868
  85.0 50.0 %all-reduce.6.cloned.1.call-start = ((), (), s32[]{:S(2)}) async-start(), calls=%async_computation.1 | async-start | bytes 393216 | tf_op jit(solution)/shard_map/psum | solution.py:116
  118.3 64.1 %all-reduce.8.cloned.1.call-start = ((), (), s32[]{:S(2)}) async-start(), calls=%async_computation.2 | async-start | bytes 393216 | tf_op jit(solution)/shard_map/psum | solution.py:122
  155.0 27.4 %copy-start.2 = (f32[16,3072]{1,0:T(8,128)S(1)}, f32[16,3072]{1,0:T(8,128)}, u32[]{:S(2)}) copy-start(f32[16,3072]{1,0:T(8,128)} %all-reduce.6.cloned.1.call-done) | copy-start | bytes 589828
Sparse Core Ops, SparseCore 0:
  85.2 26.2 all-reduce.3
  118.4 16.6 all-reduce.5
  165.7 16.6 all-reduce.7

commit v2 on v1

--- a/solution.py
+++ b/solution.py
@@ -45,7 +45,7 @@
     return rows(q_new), rows(k_new), rows(v_new)
 
 
-def attend_kernel(pos_ref, q_ref, kn_ref, vn_ref, k_ref, v_ref, ko_ref, vo_ref, o_ref, ml_ref, kt_ref, vt_ref):
+def attend_kernel(pos_ref, q_ref, kn_ref, vn_ref, k_ref, v_ref, ko_ref, vo_ref, om_ref, kt_ref, vt_ref):
     b = pl.program_id(0)
     rows, heads, dim, block = q_ref.shape[0], k_ref.shape[1], k_ref.shape[2], k_ref.shape[3]
     width = heads * dim
@@ -84,11 +84,17 @@
     weights = jnp.where(in_window, jnp.exp(scores - row_max), 0.0)
     row_sum = jnp.sum(weights, axis=1, keepdims=True)
     acc = lax.dot_general(weights.astype(jnp.bfloat16), vo_ref[0].reshape(width, block), (((1,), (1,)), ((), ())), preferred_element_type=jnp.float32)
-    o_ref[pl.ds(b, 1), :] = jnp.sum(jnp.where(own, acc, 0.0), axis=0, keepdims=True)
+    o_row = jnp.sum(jnp.where(own, acc, 0.0), axis=0, keepdims=True)
     lane_ids = lax.broadcasted_iota(jnp.int32, (heads, 128), 1)
     head_ids = lax.broadcasted_iota(jnp.int32, (heads, 128), 0)
-    stats = jnp.where(lane_ids == head_ids, row_max, 0.0) + jnp.where(lane_ids == head_ids + heads, row_sum, 0.0)
-    ml_ref[pl.ds(b, 1), :] = jnp.sum(stats, axis=0, keepdims=True)
+    half, half_width = heads // 2, width // 2
+    for core in range(2):
+        mine = head_ids - core * half
+        keep = (mine >= 0) & (mine < half)
+        stats = jnp.where(keep & (lane_ids == mine), row_max, 0.0) + jnp.where(keep & (lane_ids == mine + half), row_sum, 0.0)
+        row = jnp.concatenate([o_row[:, core * half_width:(core + 1) * half_width], jnp.sum(stats, axis=0, keepdims=True)], axis=1)
+        at_row = lax.broadcasted_iota(jnp.int32, (rows, half_width + 128), 0) == b
+        om_ref[core] = jnp.where(at_row, row, om_ref[core])
 
 
 def attend(positions, q_rows, k_rows, v_rows, k_t, v_t):
@@ -98,12 +104,12 @@
     cache = pl.BlockSpec((1, heads, dim, block), lambda b, pos: (b, 0, 0, 0))
     return pl.pallas_call(
         attend_kernel,
-        out_shape=(jax.ShapeDtypeStruct(k_t.shape, k_t.dtype), jax.ShapeDtypeStruct(v_t.shape, v_t.dtype), jax.ShapeDtypeStruct((rows, width), jnp.float32), jax.ShapeDtypeStruct((rows, 128), jnp.float32)),
+        out_shape=(jax.ShapeDtypeStruct(k_t.shape, k_t.dtype), jax.ShapeDtypeStruct(v_t.shape, v_t.dtype), jax.ShapeDtypeStruct((2, rows, width // 2 + 128), jnp.float32)),
         grid_spec=pltpu.PrefetchScalarGridSpec(
             num_scalar_prefetch=1,
             grid=(rows,),
             in_specs=[full((rows, width))] * 3 + [cache] * 2,
-            out_specs=(cache, cache, full((rows, width)), full((rows, 128))),
+            out_specs=(cache, cache, pl.BlockSpec((2, rows, width // 2 + 128), lambda b, pos: (0, 0, 0))),
             scratch_shapes=[pltpu.VMEM((width, 128), jnp.float32)] * 2,
         ),
         compiler_params=pltpu.CompilerParams(dimension_semantics=("arbitrary",), vmem_limit_bytes=48 << 20),
@@ -111,16 +117,165 @@
     )(positions, q_rows, k_rows, v_rows, k_t, v_t)
 
 
-def layer_tail(resid_in, attended, norm_mlp, w_out, w_gate_up, w_down):
-    out_part = jnp.dot(attended, w_out, preferred_element_type=jnp.float32).astype(jnp.bfloat16).astype(jnp.float32)
-    mid_resid = resid_in + lax.psum(out_part, 'tp')
-    normed_mlp = rms_norm(mid_resid, norm_mlp).astype(jnp.bfloat16)
-    gate_up = jnp.dot(normed_mlp, w_gate_up, preferred_element_type=jnp.float32)
-    ffn_local = w_down.shape[0]
-    act_vals = (jax.nn.silu(gate_up[:, :ffn_local]) * gate_up[:, ffn_local:]).astype(jnp.bfloat16)
-    down_part = jnp.dot(act_vals, w_down, preferred_element_type=jnp.float32).astype(jnp.bfloat16).astype(jnp.float32)
-    result = mid_resid + lax.psum(down_part, 'tp')
-    return result.astype(jnp.bfloat16)
+COLS = 512
+
+
+def tail_kernel(dim, om_ref, hid_ref, gain_ref, wo_hbm, wgu_hbm, wd_hbm, out_ref,
+                obuf, wo, wg, wu, wd, o_cat, snd, own, got, ysnd, ygot, x1, r2, act, x2,
+                w_sem, gu_sem, o_send, o_recv, p_send, p_recv, y_send, y_recv, g_send, g_recv):
+    tp, sp = lax.axis_index('tp'), lax.axis_index('sp')
+    core = lax.rem(sp, 2)
+    partner = sp + 1 - 2 * core
+    rows = hid_ref.shape[0]
+    half_width = wo.shape[1]
+    n_half = x1.shape[0] // 2
+    n_gu, n_wd = wg.shape[0], wd.shape[0]
+    units = wd.shape[1]
+    ffn = wgu_hbm.shape[1] // 2
+
+    def column(index):
+        side = 1 - core if index < n_half else core
+        return pl.ds(pl.multiple_of((side * n_half + index % n_half) * COLS, COLS), COLS)
+
+    weight_copies = []
+    for i in range(n_wd):
+        weight_copies.append(pltpu.make_async_copy(wo_hbm.at[pl.ds(core * half_width, half_width), column(i)], wo.at[i], w_sem.at[i]))
+    gate_up_copies = []
+    for i in range(n_gu):
+        first = core * units + i * COLS
+        gate_up_copies.append(pltpu.make_async_copy(wgu_hbm.at[:, pl.ds(pl.multiple_of(first, COLS), COLS)], wg.at[i], gu_sem.at[0, i]))
+        gate_up_copies.append(pltpu.make_async_copy(wgu_hbm.at[:, pl.ds(pl.multiple_of(ffn + first, COLS), COLS)], wu.at[i], gu_sem.at[1, i]))
+    down_copies = []
+    for i in range(n_wd):
+        down_copies.append(pltpu.make_async_copy(wd_hbm.at[pl.ds(core * units, units), column(i)], wd.at[i], w_sem.at[n_wd + i]))
+    for copy in weight_copies + gate_up_copies + down_copies:
+        copy.start()
+
+    barrier = pltpu.get_barrier_semaphore()
+    for step in range(1, 4):
+        pl.semaphore_signal(barrier, inc=1, device_id={'sp': lax.rem(sp + step, 4)}, device_id_type=MESH)
+    pl.semaphore_signal(barrier, inc=1, device_id={'tp': 1 - tp}, device_id_type=MESH)
+    pl.semaphore_wait(barrier, 4)
+
+    sent = []
+
+    def send(src, dst, send_sem, recv_sem, where):
+        copy = pltpu.make_async_remote_copy(src_ref=src, dst_ref=dst, send_sem=send_sem, recv_sem=recv_sem, device_id=where, device_id_type=MESH)
+        copy.start()
+        sent.append(copy)
+        return copy
+
+    o_copies = []
+    for step in (2, 1, 3):
+        peer = lax.rem(sp + step, 4)
+        o_copies.append(send(om_ref.at[lax.rem(peer, 2)], obuf.at[sp], o_send.at[step - 1], o_recv.at[step - 1], {'sp': peer}))
+    obuf[sp] = om_ref[core]
+    for copy in o_copies:
+        copy.wait_recv()
+
+    heads = half_width // dim
+    stats = [obuf[s, :, half_width:] for s in range(4)]
+    top = functools.reduce(jnp.maximum, stats)
+    alphas = [jnp.exp(st - top) for st in stats]
+    total = functools.reduce(lambda a, b: a + b, [al * pltpu.roll(st, 128 - heads, 1) for al, st in zip(alphas, stats)])
+    betas = [al / total for al in alphas]
+    lane = lax.broadcasted_iota(jnp.int32, (rows, 128), 1)
+    for k in range(half_width // 128):
+        first, last = 128 * k // dim, (128 * k + 127) // dim
+        value = None
+        for s in range(4):
+            scale = jnp.broadcast_to(betas[s][:, first:first + 1], (rows, 128))
+            for h in range(first + 1, last + 1):
+                scale = jnp.where(lane >= h * dim - 128 * k, betas[s][:, h:h + 1], scale)
+            term = scale * obuf[s, :, 128 * k:128 * (k + 1)]
+            value = term if value is None else value + term
+        o_cat[:, 128 * k:128 * (k + 1)] = value.astype(jnp.bfloat16)
+
+    def reduce_and_spread(stage, lhs_ref, w_ref, w_waits, base_of, dst):
+        lhs = lhs_ref[...]
+        first = []
+        for j in range(n_half):
+            w_waits[j].wait()
+            snd[stage, j] = jnp.dot(lhs, w_ref[j], preferred_element_type=jnp.float32)
+            first.append(send(snd.at[stage, j], got.at[stage, j], p_send.at[stage, j], p_recv.at[stage, j], {'sp': partner}))
+        for j in range(n_half):
+            w_waits[n_half + j].wait()
+            own[j] = jnp.dot(lhs, w_ref[n_half + j], preferred_element_type=jnp.float32)
+        second = []
+        for j in range(n_half):
+            first[j].wait_recv()
+            ysnd[stage, j] = (own[j] + got[stage, j]).astype(jnp.bfloat16).astype(jnp.float32)
+            second.append(send(ysnd.at[stage, j], ygot.at[stage, j], y_send.at[stage, j], y_recv.at[stage, j], {'tp': 1 - tp}))
+        third = []
+        for j in range(n_half):
+            second[j].wait_recv()
+            dst[core * n_half + j] = base_of(j) + (ysnd[stage, j] + ygot[stage, j])
+            third.append(send(dst.at[core * n_half + j], dst.at[core * n_half + j], g_send.at[stage, j], g_recv.at[stage, j], {'sp': partner}))
+        for copy in third:
+            copy.wait_recv()
+
+    reduce_and_spread(0, o_cat, wo, weight_copies, lambda j: hid_ref[:, column(n_half + j)].astype(jnp.float32), x1)
+
+    square = functools.reduce(lambda a, b: a + b, [x1[i] * x1[i] for i in range(2 * n_half)])
+    inv = lax.rsqrt(jnp.sum(square, axis=1, keepdims=True) / (2 * n_half * COLS) + NORM_EPS)
+    for i in range(2 * n_half):
+        cut = slice(i * COLS, (i + 1) * COLS)
+        r2[:, cut] = (x1[i] * inv * gain_ref[:, cut]).astype(jnp.bfloat16)
+
+    for i in range(n_gu):
+        gate_up_copies[2 * i].wait()
+        gate_up_copies[2 * i + 1].wait()
+        gate = jnp.dot(r2[...], wg[i], preferred_element_type=jnp.float32)
+        up = jnp.dot(r2[...], wu[i], preferred_element_type=jnp.float32)
+        act[:, i * COLS:(i + 1) * COLS] = (gate * jax.nn.sigmoid(gate) * up).astype(jnp.bfloat16)
+
+    reduce_and_spread(1, act, wd, down_copies, lambda j: x1[core * n_half + j], x2)
+    for i in range(2 * n_half):
+        out_ref[:, i * COLS:(i + 1) * COLS] = x2[i]
+    for copy in sent:
+        copy.wait_send()
+
+
+def layer_tail(om, hidden, norm_mlp, w_out, w_gate_up, w_down, dim):
+    rows, model = hidden.shape
+    half_width, units = w_out.shape[0] // 2, w_down.shape[0] // 2
+    n_wd, n_gu = model // COLS, units // COLS
+    n_half = n_wd // 2
+    f32, bf16 = jnp.float32, jnp.bfloat16
+    vmem = pl.BlockSpec(memory_space=pltpu.VMEM)
+    hbm = pl.BlockSpec(memory_space=pl.ANY)
+    dma = pltpu.SemaphoreType.DMA
+    out = pl.pallas_call(
+        functools.partial(tail_kernel, dim),
+        out_shape=jax.ShapeDtypeStruct((rows, model), f32),
+        in_specs=[vmem, vmem, vmem, hbm, hbm, hbm],
+        out_specs=vmem,
+        scratch_shapes=[
+            pltpu.VMEM((4, rows, half_width + 128), f32),
+            pltpu.VMEM((n_wd, half_width, COLS), bf16),
+            pltpu.VMEM((n_gu, model, COLS), bf16),
+            pltpu.VMEM((n_gu, model, COLS), bf16),
+            pltpu.VMEM((n_wd, units, COLS), bf16),
+            pltpu.VMEM((rows, half_width), bf16),
+            pltpu.VMEM((2, n_half, rows, COLS), f32),
+            pltpu.VMEM((n_half, rows, COLS), f32),
+            pltpu.VMEM((2, n_half, rows, COLS), f32),
+            pltpu.VMEM((2, n_half, rows, COLS), f32),
+            pltpu.VMEM((2, n_half, rows, COLS), f32),
+            pltpu.VMEM((n_wd, rows, COLS), f32),
+            pltpu.VMEM((rows, model), bf16),
+            pltpu.VMEM((rows, units), bf16),
+            pltpu.VMEM((n_wd, rows, COLS), f32),
+            dma((2 * n_wd,)), dma((2, n_gu)),
+            dma((3,)), dma((3,)),
+            dma((2, n_half)), dma((2, n_half)),
+            dma((2, n_half)), dma((2, n_half)),
+            dma((2, n_half)), dma((2, n_half)),
+        ],
+        compiler_params=pltpu.CompilerParams(collective_id=0, has_side_effects=True, vmem_limit_bytes=54 << 20),
+        name="tail",
+    )(om, hidden, norm_mlp[None, :], w_out, w_gate_up, w_down)
+    return out.astype(bf16)
 
 
 def solution(mesh):
@@ -129,13 +284,8 @@
     def local_step(hidden, positions, norm_attn, norm_mlp, w_qkv, w_out, w_gate_up, w_down, k_cache, v_cache):
         num_rows, block_len, kv_local, head_dim = k_cache.shape
         q_rows, k_rows, v_rows = new_entries(hidden, positions, norm_attn, w_qkv, kv_local, head_dim)
-        k_upd, v_upd, o_part, stats = attend(positions, q_rows, k_rows, v_rows, k_cache.transpose(0, 2, 3, 1), v_cache.transpose(0, 2, 3, 1))
-        row_max, row_sum = stats[:, :kv_local], stats[:, kv_local:2 * kv_local]
-        alpha = jnp.exp(row_max - lax.pmax(row_max, 'sp'))
-        total = lax.psum(alpha * row_sum, 'sp')
-        acc = lax.psum(o_part.reshape(num_rows, kv_local, head_dim) * alpha[..., None], 'sp')
-        attended = (acc / total[..., None]).astype(jnp.bfloat16).reshape(num_rows, -1)
-        result = layer_tail(hidden.astype(jnp.float32), attended, norm_mlp, w_out, w_gate_up, w_down)
+        k_upd, v_upd, om = attend(positions, q_rows, k_rows, v_rows, k_cache.transpose(0, 2, 3, 1), v_cache.transpose(0, 2, 3, 1))
+        result = layer_tail(om, hidden, norm_mlp, w_out, w_gate_up, w_down, head_dim)
         return result, k_upd.transpose(0, 3, 1, 2), v_upd.transpose(0, 3, 1, 2)
 
     return jax.shard_map(local_step, mesh=mesh, in_specs=(P('dp', None), P('dp'), P(None), P(None), P(None, 'tp'), P('tp', None), P(None, 'tp'), P('tp', None), cache_spec, cache_spec), out_specs=(P('dp', None), cache_spec, cache_spec), check_vma=False)

time: 191 us -> 97.2 us (0.51)
  waiting for transfers between devices: 53.8 us -> 0 us
  matrix products: 46.2 us -> 11.1 us
  Pallas kernels: 51.7 us -> 78.9 us
  blocking collectives: 15.7 us -> 0 us
  between operations: 13.9 us -> 0.71 us
  other arithmetic: 6.73 us -> 3.86 us
    psum x3 -> x0, waiting for transfers between devices: 53.8 us -> none  [the longest x1 20.4 us: local_step(): lax.psum(o_part.reshape(num_rows, kv_local, head_dim) * alpha[..., None],...]
    dot_general x3 -> x0, matrix products: 35.1 us -> none  [the longest x1 18.8 us: layer_tail(): gate_up = jnp.dot(normed_mlp, w_gate_up, preferred_element_type=jnp.float32)]
    pallas_call x0 -> x1, Pallas kernels: none -> 29 us  [layer_tail(): pl.pallas_call(functools.partial(tail_kernel, dim), out_shape=jax.ShapeDt...]
    pmax x1 -> x0, blocking collectives: 9.83 us -> none  [local_step(): alpha = jnp.exp(row_max - lax.pmax(row_max, 'sp'))]
    psum x1 -> x0, blocking collectives: 5.86 us -> none  [local_step(): total = lax.psum(alpha * row_sum, 'sp')]
  transfers between devices with their start and end apart: 3 -> 0, of which waited for: 3 -> 0; matrix products, arithmetic and copies ran while one was open for 0% -> 0% of each run, Pallas kernels for 0% -> 0%
where the time goes in v2:
time: 97.2 us; the launch traced here: 97.1 us
  Pallas kernels  78.9 us (81%)
  matrix products  11.1 us (11%)
  other arithmetic  3.86 us (4%)
  local copies, waits for them, and re-layouts  2.6 us (3%)
    pallas_call x1, Pallas kernels, attend(): pl.pallas_call(attend_kernel, out_shape=(jax.ShapeDtypeStruct(k_t.shape,...  49.9 us
    pallas_call x1, Pallas kernels, layer_tail(): pl.pallas_call(functools.partial(tail_kernel, dim), out_shape=jax.ShapeDt...  29 us
    dot_general x1, matrix products, new_entries(): jnp.dot(normed, w_qkv, preferred_element_type=jnp.float32)  11.1 us

profile of v2, /device:TPU:0, one launch (start us, length us, event | category | flops | bytes accessed | tf_op | source)
XLA Modules:
  0.0 97.1 jit_solution(9498752901772667007)
XLA Ops:
  0.6 0.0 copy-start.1
  0.6 0.7 convert_element_type.21
  1.4 1.0 %fusion = f32[16]{0:T(128)S(1)} fusion(bf16[16,3072]{1,0:T(8,128)(2,1)} %hid_ref.1), kind=kLoop, calls=%fused_computation.2 | loop fusion | flops 147440 | bytes 98368 | tf_op jit(solution)/shard_map/reduce_sum | solution.py:18
  2.4 0.1 broadcast_multiply_fusion
  2.5 0.1 fusion.8
  2.6 0.1 mul.98
  2.7 11.1 %fusion.3 = f32[16,4608]{1,0:T(8,128)S(1)} fusion(bf16[3072,4608]{1,0:T(8,128)(2,1)} %param.14, bf16[16,3072]{1,0:T(8,128)(2,1)} %hid_ref.1, f32[3072]{0:T(1024)} %param.12, f32[16]{0:T(128)S(1)} %add_rsqrt_fusion), kind=kOutput, calls=%fused_computation.10 | convolution fusion | flops 453181440 | bytes 28717120 | tf_op jit(solution)/shard_map/dot_general | solution.py:39
  13.8 0.4 reshape.89
  14.3 0.9 slice_reduce_fusion
  15.2 0.1 reshape_squeeze.3.vn_ref
  15.3 0.1 squeeze.12
  15.4 0.1 squeeze.10
  15.5 0.1 slice_negate_fusion
  15.6 0.1 maximum_multiply_fusion.1
  15.8 0.1 mul.105
  15.9 0.1 mul.102
  16.0 0.0 copy-done.1
  16.0 49.9 %attend.1 = (bf16[16,16,96,768]{3,2,1,0:T(8,128)(2,1)}, bf16[16,16,96,768]{3,2,1,0:T(8,128)(2,1)}, f32[2,16,896]{2,1,0:T(8,128)S(1)}) custom-call(s32[16]{0:T(128)S(1)} %copy-done.1, f32[16,1536]{1,0:T(8,128)S(1)} %get-tuple-element.18.q_ref, f32[16,1536]{1,0:T(8,128)S(1)} %get-tuple-element.17.kn_ref, f32[16,1536]{1,0:T(8,128)S(1)} %reshape_squeeze.3.vn_ref, ...), custom_call_target="tpu_custom_call" | custom-call | tf_op jit(solution)/shard_map/attend/pallas_call | solution.py:105
  65.9 0.0 copy-start
  65.9 0.6 copy-done
  66.5 29.0 %tail.1 = f32[16,3072]{1,0:T(8,128)} custom-call(f32[2,16,896]{2,1,0:T(8,128)} %copy-done, bf16[16,3072]{1,0:T(8,128)(2,1)} %hid_ref.1, f32[1,3072]{1,0:T(1,128)} %bitcast.19, bf16[1536,3072]{1,0:T(8,128)(2,1)} %wo_hbm.1, bf16[3072,8192]{1,0:T(8,128)(2,1)} %wgu_hbm.1, bf16[4096,3072]{1,0:T(8,128)(2,1)} %wd_hbm.1), custom_call_target="tpu_custom_call" | custom-call | tf_op jit(solution)/shard_map/tail/pallas_call | solution.py:248
  95.5 1.6 %convert_element_type.23 = bf16[16,3072]{1,0:T(8,128)(2,1)} convert(f32[16,3072]{1,0:T(8,128)} %tail.1) | non-fusion elementwise | flops 49152 | bytes 294912 | tf_op jit(solution)/shard_map/convert_element_type | solution.py:278
  (4 shorter events, 0.1 us)
Async XLA Ops:
  0.6 15.4 %copy-start.1 = (s32[16]{0:T(128)S(1)}, s32[16]{0:T(128)}, u32[]{:S(2)}) copy-start(s32[16]{0:T(128)} %pos_ref.1) | copy-start | bytes 196
  65.9 0.6 copy-start

commit v3 on v2

--- a/solution.py
+++ b/solution.py
@@ -2,6 +2,7 @@
 
 import jax
 import jax.numpy as jnp
+import numpy as np
 from jax import lax
 from jax.experimental import pallas as pl
 from jax.experimental.pallas import tpu as pltpu
@@ -14,107 +15,156 @@
 MESH = pl.DeviceIdType.MESH
 
 
-def rms_norm(values, gain_vec):
-    mean_sq = jnp.mean(values * values, axis=-1, keepdims=True)
-    return values * lax.rsqrt(mean_sq + NORM_EPS) * gain_vec
-
-
-def rope_tables(positions, head_dim):
-    inv_freq = ROPE_BASE ** (-jnp.arange(0, head_dim, 2).astype(jnp.float32) / head_dim)
-    angles = positions.astype(jnp.float32)[:, None] * inv_freq[None, :]
-    angles = jnp.concatenate([angles, angles], axis=-1)
-    return jnp.cos(angles), jnp.sin(angles)
-
-
-def rotate_half(values, cos_tab, sin_tab):
-    half_dim = values.shape[-1] // 2
-    turned = jnp.concatenate([-values[..., half_dim:], values[..., :half_dim]], axis=-1)
-    return values * cos_tab + turned * sin_tab
-
-
-def new_entries(hidden, positions, norm_attn, w_qkv, kv_count, head_dim):
-    num_rows = hidden.shape[0]
-    resid_in = hidden.astype(jnp.float32)
-    normed = rms_norm(resid_in, norm_attn).astype(jnp.bfloat16)
-    qkv_proj = jnp.dot(normed, w_qkv, preferred_element_type=jnp.float32).reshape(num_rows, kv_count, 3, head_dim)
-    cos_tab, sin_tab = rope_tables(positions, head_dim)
-    q_new = rotate_half(qkv_proj[:, :, 0], cos_tab[:, None], sin_tab[:, None])
-    k_new = rotate_half(qkv_proj[:, :, 1], cos_tab[:, None], sin_tab[:, None])
-    v_new = qkv_proj[:, :, 2]
-    rows = lambda x: x.reshape(num_rows, -1)
-    return rows(q_new), rows(k_new), rows(v_new)
-
-
-def attend_kernel(pos_ref, q_ref, kn_ref, vn_ref, k_ref, v_ref, ko_ref, vo_ref, om_ref, kt_ref, vt_ref):
-    b = pl.program_id(0)
-    rows, heads, dim, block = q_ref.shape[0], k_ref.shape[1], k_ref.shape[2], k_ref.shape[3]
+QKV_COLS = 384
+SLOTS = 8
+W_SLOTS = 4
+
+
+def attend_kernel(pos_ref, hid_ref, gain_ref, freq_ref, w_hbm, k_hbm, v_hbm, ko_hbm, vo_hbm, om_ref,
+                  k_buf, v_buf, w_buf, normed_ref, qkv_t, q_t, q_rows, in_sem, out_sem, w_sem):
+    rows, model = hid_ref.shape
+    heads, dim, block = k_buf.shape[1:]
     width = heads * dim
-
-    @pl.when(b == 0)
-    def _():
-        pad = jnp.zeros((128 - rows, width), jnp.float32)
-        kt_ref[...] = jnp.concatenate([kn_ref[...], pad], axis=0).T
-        vt_ref[...] = jnp.concatenate([vn_ref[...], pad], axis=0).T
-
+    n_w = w_hbm.shape[1] // QKV_COLS
     base = lax.axis_index('sp') * block
-    pos = pos_ref[b]
-    slot = pos - base
-    ko_ref[...] = k_ref[...]
-    vo_ref[...] = v_ref[...]
-
-    @pl.when((slot >= 0) & (slot < block))
-    def _():
-        lane = lax.rem(slot, 128)
-        start = pl.multiple_of(slot - lane, 128)
-        shift = lax.rem(lane - b + 128, 128)
-        hit = lax.broadcasted_iota(jnp.int32, (width, 128), 1) == lane
-        for new_ref, out_ref in ((kt_ref, ko_ref), (vt_ref, vo_ref)):
-            entry = pltpu.roll(new_ref[...], shift, 1)
-            old = out_ref[0, :, :, pl.ds(start, 128)].reshape(width, 128).astype(jnp.float32)
-            out_ref[0, :, :, pl.ds(start, 128)] = jnp.where(hit, entry, old).astype(jnp.bfloat16).reshape(heads, dim, 128)
+
+    def w_copy(i):
+        return pltpu.make_async_copy(w_hbm.at[:, pl.ds(i * QKV_COLS, QKV_COLS)], w_buf.at[i % W_SLOTS], w_sem.at[i % W_SLOTS])
+
+    def load(b, which):
+        slot = lax.rem(b, SLOTS)
+        src, buf = ((k_hbm, k_buf), (v_hbm, v_buf))[which]
+        return pltpu.make_async_copy(src.at[b], buf.at[slot], in_sem.at[which, slot])
+
+    def store(b, which):
+        slot = lax.rem(b, SLOTS)
+        dst, buf = ((ko_hbm, k_buf), (vo_hbm, v_buf))[which]
+        return pltpu.make_async_copy(buf.at[slot], dst.at[b], out_sem.at[which, slot])
+
+    for i in range(W_SLOTS):
+        w_copy(i).start()
+
+    resid = hid_ref[...].astype(jnp.float32)
+    inv = lax.rsqrt(jnp.sum(resid * resid, axis=1, keepdims=True) / model + NORM_EPS)
+    normed_ref[...] = (resid * inv * gain_ref[...]).astype(jnp.bfloat16)
+    pad = jnp.zeros((128 - rows, QKV_COLS), jnp.float32)
+    for i in range(n_w):
+        w_copy(i).wait()
+        part = jnp.dot(normed_ref[...], w_buf[i % W_SLOTS], preferred_element_type=jnp.float32)
+        if i + W_SLOTS < n_w:
+            w_copy(i + W_SLOTS).start()
+        elif i + W_SLOTS < n_w + SLOTS:
+            load(i + W_SLOTS - n_w, 0).start()
+            load(i + W_SLOTS - n_w, 1).start()
+        qkv_t[i * QKV_COLS:(i + 1) * QKV_COLS, :] = jnp.concatenate([part, pad], axis=0).T
+    for b in range(W_SLOTS, SLOTS):
+        load(b, 0).start()
+        load(b, 1).start()
+
+    lane = lax.broadcasted_iota(jnp.int32, (1, 128), 1)
+    pos_row = jnp.zeros((1, 128), jnp.int32)
+    for b in range(rows):
+        pos_row = jnp.where(lane == b, pos_ref[b], pos_row)
+    angles = pos_row.astype(jnp.float32) * freq_ref[...]
+    cos_t, sin_t = jnp.cos(angles), jnp.sin(angles)
+    half = dim // 2
+    for h in range(heads):
+        for part in range(2):
+            first = (3 * h + part) * dim
+            low, high = qkv_t[first:first + half, :], qkv_t[first + half:first + dim, :]
+            dst, at = (q_t, h * dim) if part == 0 else (qkv_t, first)
+            dst[at:at + half, :] = low * cos_t - high * sin_t
+            dst[at + half:at + dim, :] = high * cos_t + low * sin_t
+    q_rows[...] = q_t[...].T[:rows, :]
 
     own = lax.broadcasted_iota(jnp.int32, (heads, width), 1) // dim == lax.broadcasted_iota(jnp.int32, (heads, width), 0)
-    q_row = jnp.broadcast_to(q_ref[pl.ds(b, 1), :], (heads, width))
-    q_diag = jnp.where(own, q_row, 0.0).astype(jnp.bfloat16)
-    scores = jnp.dot(q_diag, ko_ref[0].reshape(width, block), preferred_element_type=jnp.float32) * (dim ** -0.5)
-    slot_ids = lax.broadcasted_iota(jnp.int32, (heads, block), 1) + base
-    in_window = (slot_ids <= pos) & (slot_ids >= pos - WINDOW)
-    scores = jnp.where(in_window, scores, NEG)
-    row_max = jnp.max(scores, axis=1, keepdims=True)
-    weights = jnp.where(in_window, jnp.exp(scores - row_max), 0.0)
-    row_sum = jnp.sum(weights, axis=1, keepdims=True)
-    acc = lax.dot_general(weights.astype(jnp.bfloat16), vo_ref[0].reshape(width, block), (((1,), (1,)), ((), ())), preferred_element_type=jnp.float32)
-    o_row = jnp.sum(jnp.where(own, acc, 0.0), axis=0, keepdims=True)
     lane_ids = lax.broadcasted_iota(jnp.int32, (heads, 128), 1)
     head_ids = lax.broadcasted_iota(jnp.int32, (heads, 128), 0)
-    half, half_width = heads // 2, width // 2
-    for core in range(2):
-        mine = head_ids - core * half
-        keep = (mine >= 0) & (mine < half)
-        stats = jnp.where(keep & (lane_ids == mine), row_max, 0.0) + jnp.where(keep & (lane_ids == mine + half), row_sum, 0.0)
-        row = jnp.concatenate([o_row[:, core * half_width:(core + 1) * half_width], jnp.sum(stats, axis=0, keepdims=True)], axis=1)
-        at_row = lax.broadcasted_iota(jnp.int32, (rows, half_width + 128), 0) == b
-        om_ref[core] = jnp.where(at_row, row, om_ref[core])
-
-
-def attend(positions, q_rows, k_rows, v_rows, k_t, v_t):
+    half_heads, half_width = heads // 2, width // 2
+
+    def patch(buf, slot, which, b, pos):
+        at = pos - base
+
+        @pl.when((at >= 0) & (at < block))
+        def _():
+            inner = lax.rem(at, 128)
+            start = pl.multiple_of(at - inner, 128)
+            shift = lax.rem(inner - b + 128, 128)
+            hit = lax.broadcasted_iota(jnp.int32, (dim, 128), 1) == inner
+            for h in range(heads):
+                first = (3 * h + 1 + which) * dim
+                entry = pltpu.roll(qkv_t[first:first + dim, :], shift, 1)
+                old = buf[slot, h, :, pl.ds(start, 128)].astype(jnp.float32)
+                buf[slot, h, :, pl.ds(start, 128)] = jnp.where(hit, entry, old).astype(jnp.bfloat16)
+
+    def step(b, carry):
+        slot = lax.rem(b, SLOTS)
+        pos = pos_ref[b]
+
+        @pl.when((b >= 2) & (b + SLOTS - 2 < rows))
+        def _():
+            for which in range(2):
+                store(b - 2, which).wait()
+                load(b + SLOTS - 2, which).start()
+
+        load(b, 0).wait()
+        patch(k_buf, slot, 0, b, pos)
+        store(b, 0).start()
+        q_row = jnp.broadcast_to(q_rows[pl.ds(b, 1), :], (heads, width))
+        q_diag = jnp.where(own, q_row, 0.0).astype(jnp.bfloat16)
+        scores = jnp.dot(q_diag, k_buf[slot].reshape(width, block), preferred_element_type=jnp.float32) * (dim ** -0.5)
+        slot_ids = lax.broadcasted_iota(jnp.int32, (heads, block), 1) + base
+        in_window = (slot_ids <= pos) & (slot_ids >= pos - WINDOW)
+        scores = jnp.where(in_window, scores, NEG)
+        row_max = jnp.max(scores, axis=1, keepdims=True)
+        weights = jnp.where(in_window, jnp.exp(scores - row_max), 0.0)
+        row_sum = jnp.sum(weights, axis=1, keepdims=True)
+        load(b, 1).wait()
+        patch(v_buf, slot, 1, b, pos)
+        store(b, 1).start()
+        acc = lax.dot_general(weights.astype(jnp.bfloat16), v_buf[slot].reshape(width, block), (((1,), (1,)), ((), ())), preferred_element_type=jnp.float32)
+        o_row = jnp.sum(jnp.where(own, acc, 0.0), axis=0, keepdims=True)
+        for core in range(2):
+            mine = head_ids - core * half_heads
+            keep = (mine >= 0) & (mine < half_heads)
+            stats = jnp.where(keep & (lane_ids == mine), row_max, 0.0) + jnp.where(keep & (lane_ids == mine + half_heads), row_sum, 0.0)
+            row = jnp.concatenate([o_row[:, core * half_width:(core + 1) * half_width], jnp.sum(stats, axis=0, keepdims=True)], axis=1)
+            at_row = lax.broadcasted_iota(jnp.int32, (rows, half_width + 128), 0) == b
+            om_ref[core] = jnp.where(at_row, row, om_ref[core])
+        return carry
+
+    lax.fori_loop(0, rows, step, 0)
+    for b in range(rows - SLOTS, rows):
+        store(b, 0).wait()
+        store(b, 1).wait()
+
+
+def attend(positions, hidden, norm_attn, w_qkv, k_t, v_t):
     rows, heads, dim, block = k_t.shape
-    width = heads * dim
-    full = lambda shape: pl.BlockSpec(shape, lambda b, pos: (0, 0))
-    cache = pl.BlockSpec((1, heads, dim, block), lambda b, pos: (b, 0, 0, 0))
+    width, model = heads * dim, hidden.shape[1]
+    freq = (ROPE_BASE ** (-np.arange(0, dim, 2).astype(np.float64) / dim)).astype(np.float32)
+    freq = jnp.asarray(np.broadcast_to(freq[:, None], (dim // 2, 128)))
+    vmem = pl.BlockSpec(memory_space=pltpu.VMEM)
+    hbm = pl.BlockSpec(memory_space=pl.ANY)
+    f32, bf16, dma = jnp.float32, jnp.bfloat16, pltpu.SemaphoreType.DMA
     return pl.pallas_call(
         attend_kernel,
-        out_shape=(jax.ShapeDtypeStruct(k_t.shape, k_t.dtype), jax.ShapeDtypeStruct(v_t.shape, v_t.dtype), jax.ShapeDtypeStruct((2, rows, width // 2 + 128), jnp.float32)),
-        grid_spec=pltpu.PrefetchScalarGridSpec(
-            num_scalar_prefetch=1,
-            grid=(rows,),
-            in_specs=[full((rows, width))] * 3 + [cache] * 2,
-            out_specs=(cache, cache, pl.BlockSpec((2, rows, width // 2 + 128), lambda b, pos: (0, 0, 0))),
-            scratch_shapes=[pltpu.VMEM((width, 128), jnp.float32)] * 2,
-        ),
-        compiler_params=pltpu.CompilerParams(dimension_semantics=("arbitrary",), vmem_limit_bytes=48 << 20),
+        out_shape=(jax.ShapeDtypeStruct(k_t.shape, k_t.dtype), jax.ShapeDtypeStruct(v_t.shape, v_t.dtype), jax.ShapeDtypeStruct((2, rows, width // 2 + 128), f32)),
+        in_specs=[pl.BlockSpec(memory_space=pltpu.SMEM), vmem, vmem, vmem, hbm, hbm, hbm],
+        out_specs=(hbm, hbm, vmem),
+        scratch_shapes=[
+            pltpu.VMEM((SLOTS, heads, dim, block), bf16),
+            pltpu.VMEM((SLOTS, heads, dim, block), bf16),
+            pltpu.VMEM((W_SLOTS, model, QKV_COLS), bf16),
+            pltpu.VMEM((rows, model), bf16),
+            pltpu.VMEM((3 * width, 128), f32),
+            pltpu.VMEM((width, 128), f32),
+            pltpu.VMEM((rows, width), f32),
+            dma((2, SLOTS)), dma((2, SLOTS)), dma((W_SLOTS,)),
+        ],
+        compiler_params=pltpu.CompilerParams(vmem_limit_bytes=58 << 20),
         name="attend",
-    )(positions, q_rows, k_rows, v_rows, k_t, v_t)
+    )(positions, hidden, norm_attn[None, :], freq, w_qkv, k_t, v_t)
 
 
 COLS = 512
@@ -283,8 +333,7 @@
 
     def local_step(hidden, positions, norm_attn, norm_mlp, w_qkv, w_out, w_gate_up, w_down, k_cache, v_cache):
         num_rows, block_len, kv_local, head_dim = k_cache.shape
-        q_rows, k_rows, v_rows = new_entries(hidden, positions, norm_attn, w_qkv, kv_local, head_dim)
-        k_upd, v_upd, om = attend(positions, q_rows, k_rows, v_rows, k_cache.transpose(0, 2, 3, 1), v_cache.transpose(0, 2, 3, 1))
+        k_upd, v_upd, om = attend(positions, hidden, norm_attn, w_qkv, k_cache.transpose(0, 2, 3, 1), v_cache.transpose(0, 2, 3, 1))
         result = layer_tail(om, hidden, norm_mlp, w_out, w_gate_up, w_down, head_dim)
         return result, k_upd.transpose(0, 3, 1, 2), v_upd.transpose(0, 3, 1, 2)
 

time: 97.2 us -> 91.1 us (0.937)
  matrix products: 11.1 us -> 0 us
  Pallas kernels: 78.9 us -> 87.4 us
  other arithmetic: 3.86 us -> 1.58 us
  local copies, waits for them, and re-layouts: 2.6 us -> 1.34 us
    dot_general x1 -> x0, matrix products: 11.1 us -> none  [new_entries(): jnp.dot(normed, w_qkv, preferred_element_type=jnp.float32)]
    pallas_call x1, Pallas kernels: 49.9 us -> 60 us  [attend(): pl.pallas_call(attend_kernel, out_shape=(jax.ShapeDtypeStruct(k_t.shape,...]
    pallas_call x1, Pallas kernels: 29 us -> 27.3 us  [layer_tail(): pl.pallas_call(functools.partial(tail_kernel, dim), out_shape=jax.ShapeDt...]
    another operation x1, local copies, waits for them, and re-layouts: 0.1 us -> 1.34 us  [new_entries(): rows = lambda x: x.reshape(num_rows, -1)]
    reduce_sum x1 -> x0, other arithmetic: 1.03 us -> none  [rms_norm(): mean_sq = jnp.mean(values * values, axis=-1, keepdims=True)]
where the time goes in v3:
time: 91.1 us; the launch traced here: 90.9 us
  Pallas kernels  87.4 us (96%)
  other arithmetic  1.58 us (2%)
  local copies, waits for them, and re-layouts  1.34 us (1%)
    pallas_call x1, Pallas kernels, attend(): pl.pallas_call(attend_kernel, out_shape=(jax.ShapeDtypeStruct(k_t.shape,...  60 us
    pallas_call x1, Pallas kernels, layer_tail(): pl.pallas_call(functools.partial(tail_kernel, dim), out_shape=jax.ShapeDt...  27.3 us

profile of v3, /device:TPU:0, one launch (start us, length us, event | category | flops | bytes accessed | tf_op | source)
XLA Modules:
  0.0 90.9 jit_solution(4870164786543079072)
XLA Ops:
  0.6 1.3 %jit_solution_.3.freq_ref = f32[48,128]{1,0:T(8,128)} broadcast(f32[48]{0:T(128)} %constant.2.clone), dimensions={0} | broadcast | bytes 24768 | tf_op jit(solution)
  2.0 60.0 %attend.1 = (bf16[16,16,96,768]{3,2,1,0:T(8,128)(2,1)}, bf16[16,16,96,768]{3,2,1,0:T(8,128)(2,1)}, f32[2,16,896]{2,1,0:T(8,128)}) custom-call(s32[16]{0:T(128)} %pos_ref.1, bf16[16,3072]{1,0:T(8,128)(2,1)} %hid_ref.3, f32[1,3072]{1,0:T(1,128)} %bitcast.8, f32[48,128]{1,0:T(8,128)} %jit_solution_.3.freq_ref, bf16[3072,4608]{1,0:T(8,128)(2,1)} %w_hbm.1, ...), custom_call_target="tpu_custom_call" | custom-call | tf_op jit(solution)/shard_map/attend/pallas_call | solution.py:150
  62.0 27.3 %tail.1 = f32[16,3072]{1,0:T(8,128)} custom-call(f32[2,16,896]{2,1,0:T(8,128)} %get-tuple-element.6.om_ref, bf16[16,3072]{1,0:T(8,128)(2,1)} %hid_ref.3, f32[1,3072]{1,0:T(1,128)} %bitcast.9, bf16[1536,3072]{1,0:T(8,128)(2,1)} %wo_hbm.1, bf16[3072,8192]{1,0:T(8,128)(2,1)} %wgu_hbm.1, bf16[4096,3072]{1,0:T(8,128)(2,1)} %wd_hbm.1), custom_call_target="tpu_custom_call" | custom-call | tf_op jit(solution)/shard_map/tail/pallas_call | solution.py:298
  89.3 1.6 %convert_element_type.3 = bf16[16,3072]{1,0:T(8,128)(2,1)} convert(f32[16,3072]{1,0:T(8,128)} %tail.1) | non-fusion elementwise | flops 49152 | bytes 294912 | tf_op jit(solution)/shard_map/convert_element_type | solution.py:328

commit v4 on v3

--- a/solution.py
+++ b/solution.py
@@ -1,8 +1,8 @@
 import functools
+import math
 
 import jax
 import jax.numpy as jnp
-import numpy as np
 from jax import lax
 from jax.experimental import pallas as pl
 from jax.experimental.pallas import tpu as pltpu
@@ -16,66 +16,135 @@
 
 
 QKV_COLS = 384
-SLOTS = 8
-W_SLOTS = 4
-
-
-def attend_kernel(pos_ref, hid_ref, gain_ref, freq_ref, w_hbm, k_hbm, v_hbm, ko_hbm, vo_hbm, om_ref,
-                  k_buf, v_buf, w_buf, normed_ref, qkv_t, q_t, q_rows, in_sem, out_sem, w_sem):
+SLOTS = 7
+PRE = 6
+
+
+def project_kernel(dim, pos_hbm, hid_hbm, gain_hbm, w_hbm, k_hbm, v_hbm, rows_ref, k_ring, v_ring,
+                   pos_ref, hid_ref, gain_ref, w_buf, normed_ref, qkv_t, turned, msg, gath,
+                   w_sem, in_sem, side_sem, s_send, s_recv):
+    sp = lax.axis_index('sp')
     rows, model = hid_ref.shape
-    heads, dim, block = k_buf.shape[1:]
-    width = heads * dim
-    n_w = w_hbm.shape[1] // QKV_COLS
-    base = lax.axis_index('sp') * block
-
-    def w_copy(i):
-        return pltpu.make_async_copy(w_hbm.at[:, pl.ds(i * QKV_COLS, QKV_COLS)], w_buf.at[i % W_SLOTS], w_sem.at[i % W_SLOTS])
-
-    def load(b, which):
-        slot = lax.rem(b, SLOTS)
-        src, buf = ((k_hbm, k_buf), (v_hbm, v_buf))[which]
-        return pltpu.make_async_copy(src.at[b], buf.at[slot], in_sem.at[which, slot])
-
-    def store(b, which):
-        slot = lax.rem(b, SLOTS)
-        dst, buf = ((ko_hbm, k_buf), (vo_hbm, v_buf))[which]
-        return pltpu.make_async_copy(buf.at[slot], dst.at[b], out_sem.at[which, slot])
-
-    for i in range(W_SLOTS):
-        w_copy(i).start()
+    mine = qkv_t.shape[0]
+    n_w = mine // QKV_COLS
+    w_copies = []
+    for i in range(n_w):
+        first = pl.multiple_of(sp * mine + i * QKV_COLS, QKV_COLS)
+        w_copies.append(pltpu.make_async_copy(w_hbm.at[:, pl.ds(first, QKV_COLS)], w_buf.at[i], w_sem.at[i]))
+    side = [pltpu.make_async_copy(src, dst, side_sem.at[i]) for i, (src, dst) in enumerate(((hid_hbm, hid_ref), (gain_hbm, gain_ref), (pos_hbm, pos_ref)))]
+    loads = []
+    for b in range(PRE):
+        loads.append(pltpu.make_async_copy(k_hbm.at[b], k_ring.at[b], in_sem.at[0, b]))
+        loads.append(pltpu.make_async_copy(v_hbm.at[b], v_ring.at[b], in_sem.at[1, b]))
+    for copy in side + w_copies + loads:
+        copy.start()
+    barrier = pltpu.get_barrier_semaphore()
+    for step in range(1, 4):
+        pl.semaphore_signal(barrier, inc=1, device_id={'sp': lax.rem(sp + step, 4)}, device_id_type=MESH)
+    for copy in side:
+        copy.wait()
+
+    half = dim // 2
+    lane = lax.broadcasted_iota(jnp.int32, (1, 128), 1)
+    pos_row = jnp.zeros((1, 128), jnp.int32)
+    for b in range(rows):
+        pos_row = jnp.where(lane == b, pos_ref[b], pos_row)
+    pair = lax.broadcasted_iota(jnp.int32, (half, 128), 0).astype(jnp.float32)
+    angles = pos_row.astype(jnp.float32) * jnp.exp(pair * (-2.0 / dim * math.log(ROPE_BASE)))
+    cos_t, sin_t = jnp.cos(angles), jnp.sin(angles)
 
     resid = hid_ref[...].astype(jnp.float32)
     inv = lax.rsqrt(jnp.sum(resid * resid, axis=1, keepdims=True) / model + NORM_EPS)
     normed_ref[...] = (resid * inv * gain_ref[...]).astype(jnp.bfloat16)
     pad = jnp.zeros((128 - rows, QKV_COLS), jnp.float32)
     for i in range(n_w):
-        w_copy(i).wait()
-        part = jnp.dot(normed_ref[...], w_buf[i % W_SLOTS], preferred_element_type=jnp.float32)
-        if i + W_SLOTS < n_w:
-            w_copy(i + W_SLOTS).start()
-        elif i + W_SLOTS < n_w + SLOTS:
-            load(i + W_SLOTS - n_w, 0).start()
-            load(i + W_SLOTS - n_w, 1).start()
+        w_copies[i].wait()
+        part = jnp.dot(normed_ref[...], w_buf[i], preferred_element_type=jnp.float32)
         qkv_t[i * QKV_COLS:(i + 1) * QKV_COLS, :] = jnp.concatenate([part, pad], axis=0).T
-    for b in range(W_SLOTS, SLOTS):
+    third = mine // 3
+    for h in range(third // dim):
+        for part in range(2):
+            first = (3 * h + part) * dim
+            at = part * third + h * dim
+            low, high = qkv_t[first:first + half, :], qkv_t[first + half:first + dim, :]
+            turned[at:at + half, :] = low * cos_t - high * sin_t
+            turned[at + half:at + dim, :] = high * cos_t + low * sin_t
+        turned[2 * third + h * dim:2 * third + (h + 1) * dim, :] = qkv_t[(3 * h + 2) * dim:(3 * h + 3) * dim, :]
+    own_rows = turned[...].T[:rows, :]
+    msg[...] = own_rows
+    pl.semaphore_wait(barrier, 3)
+    sends = []
+    for step in (2, 1, 3):
+        copy = pltpu.make_async_remote_copy(src_ref=msg, dst_ref=gath.at[sp], send_sem=s_send.at[step - 1], recv_sem=s_recv.at[step - 1],
+                                            device_id={'sp': lax.rem(sp + step, 4)}, device_id_type=MESH)
+        copy.start()
+        sends.append(copy)
+    gath[sp] = own_rows
+    for copy in sends:
+        copy.wait_recv()
+    rows_ref[...] = gath[...]
+    for copy in loads:
+        copy.wait()
+    for copy in sends:
+        copy.wait_send()
+
+
+def project(positions, hidden, norm_attn, w_qkv, k_t, v_t):
+    rows, heads, dim, block = k_t.shape
+    model, mine = hidden.shape[1], w_qkv.shape[1] // 4
+    vmem = pl.BlockSpec(memory_space=pltpu.VMEM)
+    hbm = pl.BlockSpec(memory_space=pl.ANY)
+    f32, bf16, dma = jnp.float32, jnp.bfloat16, pltpu.SemaphoreType.DMA
+    return pl.pallas_call(
+        functools.partial(project_kernel, dim),
+        out_shape=(pltpu.VMEM((4, rows, mine), f32), pltpu.VMEM((SLOTS, heads, dim, block), bf16), pltpu.VMEM((SLOTS, heads, dim, block), bf16)),
+        in_specs=[hbm] * 6,
+        out_specs=(vmem, vmem, vmem),
+        scratch_shapes=[
+            pltpu.SMEM((rows,), jnp.int32),
+            pltpu.VMEM((rows, model), bf16),
+            pltpu.VMEM((1, model), f32),
+            pltpu.VMEM((mine // QKV_COLS, model, QKV_COLS), bf16),
+            pltpu.VMEM((rows, model), bf16),
+            pltpu.VMEM((mine, 128), f32),
+            pltpu.VMEM((mine, 128), f32),
+            pltpu.VMEM((rows, mine), f32),
+            pltpu.VMEM((4, rows, mine), f32),
+            dma((mine // QKV_COLS,)), dma((2, PRE)), dma((3,)), dma((3,)), dma((3,)),
+        ],
+        compiler_params=pltpu.CompilerParams(collective_id=1, has_side_effects=True, vmem_limit_bytes=14 << 20),
+        name="project",
+    )(*(pltpu.with_memory_space_constraint(x, pltpu.HBM) for x in (positions, hidden, norm_attn[None, :])), w_qkv, k_t, v_t)
+
+
+def attend_kernel(pos_hbm, rows_ref, k_in, v_in, k_hbm, v_hbm, ko_hbm, vo_hbm, om_ref, k_ring, v_ring,
+                  pos_ref, new_t, in_sem, out_sem, side_sem):
+    rows = rows_ref.shape[1]
+    heads, dim, block = k_ring.shape[1:]
+    width, third = heads * dim, rows_ref.shape[2] // 3
+    base = lax.axis_index('sp') * block
+
+    def load(b, which):
+        slot = lax.rem(b, SLOTS)
+        src, buf = ((k_hbm, k_ring), (v_hbm, v_ring))[which]
+        return pltpu.make_async_copy(src.at[b], buf.at[slot], in_sem.at[which, slot])
+
+    def store(b, which):
+        slot = lax.rem(b, SLOTS)
+        dst, buf = ((ko_hbm, k_ring), (vo_hbm, v_ring))[which]
+        return pltpu.make_async_copy(buf.at[slot], dst.at[b], out_sem.at[which, slot])
+
+    pos_copy = pltpu.make_async_copy(pos_hbm, pos_ref, side_sem)
+    pos_copy.start()
+    for b in range(PRE, SLOTS):
         load(b, 0).start()
         load(b, 1).start()
-
-    lane = lax.broadcasted_iota(jnp.int32, (1, 128), 1)
-    pos_row = jnp.zeros((1, 128), jnp.int32)
-    for b in range(rows):
-        pos_row = jnp.where(lane == b, pos_ref[b], pos_row)
-    angles = pos_row.astype(jnp.float32) * freq_ref[...]
-    cos_t, sin_t = jnp.cos(angles), jnp.sin(angles)
-    half = dim // 2
-    for h in range(heads):
-        for part in range(2):
-            first = (3 * h + part) * dim
-            low, high = qkv_t[first:first + half, :], qkv_t[first + half:first + dim, :]
-            dst, at = (q_t, h * dim) if part == 0 else (qkv_t, first)
-            dst[at:at + half, :] = low * cos_t - high * sin_t
-            dst[at + half:at + dim, :] = high * cos_t + low * sin_t
-    q_rows[...] = q_t[...].T[:rows, :]
+    pad = jnp.zeros((128 - rows, third), jnp.float32)
+    for which in range(2):
+        for s in range(4):
+            entry = rows_ref[s, :, (1 + which) * third:(2 + which) * third]
+            new_t[which, s * third:(s + 1) * third, :] = jnp.concatenate([entry, pad], axis=0).T
+    pos_copy.wait()
 
     own = lax.broadcasted_iota(jnp.int32, (heads, width), 1) // dim == lax.broadcasted_iota(jnp.int32, (heads, width), 0)
     lane_ids = lax.broadcasted_iota(jnp.int32, (heads, 128), 1)
@@ -92,8 +161,7 @@
             shift = lax.rem(inner - b + 128, 128)
             hit = lax.broadcasted_iota(jnp.int32, (dim, 128), 1) == inner
             for h in range(heads):
-                first = (3 * h + 1 + which) * dim
-                entry = pltpu.roll(qkv_t[first:first + dim, :], shift, 1)
+                entry = pltpu.roll(new_t[which, h * dim:(h + 1) * dim, :], shift, 1)
                 old = buf[slot, h, :, pl.ds(start, 128)].astype(jnp.float32)
                 buf[slot, h, :, pl.ds(start, 128)] = jnp.where(hit, entry, old).astype(jnp.bfloat16)
 
@@ -107,27 +175,34 @@
                 store(b - 2, which).wait()
                 load(b + SLOTS - 2, which).start()
 
-        load(b, 0).wait()
-        patch(k_buf, slot, 0, b, pos)
+        @pl.when(b >= PRE)
+        def _():
+            load(b, 0).wait()
+
+        patch(k_ring, slot, 0, b, pos)
         store(b, 0).start()
-        q_row = jnp.broadcast_to(q_rows[pl.ds(b, 1), :], (heads, width))
-        q_diag = jnp.where(own, q_row, 0.0).astype(jnp.bfloat16)
-        scores = jnp.dot(q_diag, k_buf[slot].reshape(width, block), preferred_element_type=jnp.float32) * (dim ** -0.5)
+        q_row = jnp.concatenate([rows_ref[s, pl.ds(b, 1), :third] for s in range(4)], axis=1)
+        q_diag = jnp.where(own, jnp.broadcast_to(q_row, (heads, width)), 0.0).astype(jnp.bfloat16)
+        scores = jnp.dot(q_diag, k_ring[slot].reshape(width, block), preferred_element_type=jnp.float32) * (dim ** -0.5)
         slot_ids = lax.broadcasted_iota(jnp.int32, (heads, block), 1) + base
         in_window = (slot_ids <= pos) & (slot_ids >= pos - WINDOW)
         scores = jnp.where(in_window, scores, NEG)
         row_max = jnp.max(scores, axis=1, keepdims=True)
         weights = jnp.where(in_window, jnp.exp(scores - row_max), 0.0)
         row_sum = jnp.sum(weights, axis=1, keepdims=True)
-        load(b, 1).wait()
-        patch(v_buf, slot, 1, b, pos)
+
+        @pl.when(b >= PRE)
+        def _():
+            load(b, 1).wait()
+
+        patch(v_ring, slot, 1, b, pos)
         store(b, 1).start()
-        acc = lax.dot_general(weights.astype(jnp.bfloat16), v_buf[slot].reshape(width, block), (((1,), (1,)), ((), ())), preferred_element_type=jnp.float32)
+        acc = lax.dot_general(weights.astype(jnp.bfloat16), v_ring[slot].reshape(width, block), (((1,), (1,)), ((), ())), preferred_element_type=jnp.float32)
         o_row = jnp.sum(jnp.where(own, acc, 0.0), axis=0, keepdims=True)
         for core in range(2):
-            mine = head_ids - core * half_heads
-            keep = (mine >= 0) & (mine < half_heads)
-            stats = jnp.where(keep & (lane_ids == mine), row_max, 0.0) + jnp.where(keep & (lane_ids == mine + half_heads), row_sum, 0.0)
+            local = head_ids - core * half_heads
+            keep = (local >= 0) & (local < half_heads)
+            stats = jnp.where(keep & (lane_ids == local), row_max, 0.0) + jnp.where(keep & (lane_ids == local + half_heads), row_sum, 0.0)
             row = jnp.concatenate([o_row[:, core * half_width:(core + 1) * half_width], jnp.sum(stats, axis=0, keepdims=True)], axis=1)
             at_row = lax.broadcasted_iota(jnp.int32, (rows, half_width + 128), 0) == b
             om_ref[core] = jnp.where(at_row, row, om_ref[core])
@@ -139,40 +214,36 @@
         store(b, 1).wait()
 
 
-def attend(positions, hidden, norm_attn, w_qkv, k_t, v_t):
+def attend(positions, new_rows, k_ring, v_ring, k_t, v_t):
     rows, heads, dim, block = k_t.shape
-    width, model = heads * dim, hidden.shape[1]
-    freq = (ROPE_BASE ** (-np.arange(0, dim, 2).astype(np.float64) / dim)).astype(np.float32)
-    freq = jnp.asarray(np.broadcast_to(freq[:, None], (dim // 2, 128)))
+    width = heads * dim
     vmem = pl.BlockSpec(memory_space=pltpu.VMEM)
     hbm = pl.BlockSpec(memory_space=pl.ANY)
     f32, bf16, dma = jnp.float32, jnp.bfloat16, pltpu.SemaphoreType.DMA
-    return pl.pallas_call(
+    ring = pltpu.VMEM((SLOTS, heads, dim, block), bf16)
+    k_upd, v_upd, om, _, _ = pl.pallas_call(
         attend_kernel,
-        out_shape=(jax.ShapeDtypeStruct(k_t.shape, k_t.dtype), jax.ShapeDtypeStruct(v_t.shape, v_t.dtype), jax.ShapeDtypeStruct((2, rows, width // 2 + 128), f32)),
-        in_specs=[pl.BlockSpec(memory_space=pltpu.SMEM), vmem, vmem, vmem, hbm, hbm, hbm],
-        out_specs=(hbm, hbm, vmem),
+        out_shape=(jax.ShapeDtypeStruct(k_t.shape, k_t.dtype), jax.ShapeDtypeStruct(v_t.shape, v_t.dtype), pltpu.VMEM((2, rows, width // 2 + 128), f32), ring, ring),
+        in_specs=[hbm, vmem, vmem, vmem, hbm, hbm],
+        out_specs=(hbm, hbm, vmem, vmem, vmem),
         scratch_shapes=[
-            pltpu.VMEM((SLOTS, heads, dim, block), bf16),
-            pltpu.VMEM((SLOTS, heads, dim, block), bf16),
-            pltpu.VMEM((W_SLOTS, model, QKV_COLS), bf16),
-            pltpu.VMEM((rows, model), bf16),
-            pltpu.VMEM((3 * width, 128), f32),
-            pltpu.VMEM((width, 128), f32),
-            pltpu.VMEM((rows, width), f32),
-            dma((2, SLOTS)), dma((2, SLOTS)), dma((W_SLOTS,)),
+            pltpu.SMEM((rows,), jnp.int32),
+            pltpu.VMEM((2, width, 128), f32),
+            dma((2, SLOTS)), dma((2, SLOTS)), dma,
         ],
-        compiler_params=pltpu.CompilerParams(vmem_limit_bytes=58 << 20),
+        input_output_aliases={2: 3, 3: 4},
+        compiler_params=pltpu.CompilerParams(vmem_limit_bytes=10 << 20),
         name="attend",
-    )(positions, hidden, norm_attn[None, :], freq, w_qkv, k_t, v_t)
+    )(pltpu.with_memory_space_constraint(positions, pltpu.HBM), *(pltpu.with_memory_space_constraint(x, pltpu.VMEM) for x in (new_rows, k_ring, v_ring)), k_t, v_t)
+    return k_upd, v_upd, om
 
 
 COLS = 512
 
 
-def tail_kernel(dim, om_ref, hid_ref, gain_ref, wo_hbm, wgu_hbm, wd_hbm, out_ref,
-                obuf, wo, wg, wu, wd, o_cat, snd, own, got, ysnd, ygot, x1, r2, act, x2,
-                w_sem, gu_sem, o_send, o_recv, p_send, p_recv, y_send, y_recv, g_send, g_recv):
+def tail_kernel(dim, om_ref, hid_hbm, gain_hbm, wo_hbm, wgu_hbm, wd_hbm, out_ref,
+                hid_ref, gain_ref, obuf, wo, wg, wu, wd, o_cat, snd, own, got, ysnd, ygot, x1, r2, act, x2,
+                side_sem, w_sem, gu_sem, o_send, o_recv, p_send, p_recv, y_send, y_recv, g_send, g_recv):
     tp, sp = lax.axis_index('tp'), lax.axis_index('sp')
     core = lax.rem(sp, 2)
     partner = sp + 1 - 2 * core
@@ -198,7 +269,8 @@
     down_copies = []
     for i in range(n_wd):
         down_copies.append(pltpu.make_async_copy(wd_hbm.at[pl.ds(core * units, units), column(i)], wd.at[i], w_sem.at[n_wd + i]))
-    for copy in weight_copies + gate_up_copies + down_copies:
+    side = [pltpu.make_async_copy(hid_hbm, hid_ref, side_sem.at[0]), pltpu.make_async_copy(gain_hbm, gain_ref, side_sem.at[1])]
+    for copy in weight_copies + side + gate_up_copies + down_copies:
         copy.start()
 
     barrier = pltpu.get_barrier_semaphore()
@@ -264,6 +336,8 @@
         for copy in third:
             copy.wait_recv()
 
+    for copy in side:
+        copy.wait()
     reduce_and_spread(0, o_cat, wo, weight_copies, lambda j: hid_ref[:, column(n_half + j)].astype(jnp.float32), x1)
 
     square = functools.reduce(lambda a, b: a + b, [x1[i] * x1[i] for i in range(2 * n_half)])
@@ -297,10 +371,12 @@
     dma = pltpu.SemaphoreType.DMA
     out = pl.pallas_call(
         functools.partial(tail_kernel, dim),
-        out_shape=jax.ShapeDtypeStruct((rows, model), f32),
-        in_specs=[vmem, vmem, vmem, hbm, hbm, hbm],
+        out_shape=pltpu.VMEM((rows, model), f32),
+        in_specs=[vmem, hbm, hbm, hbm, hbm, hbm],
         out_specs=vmem,
         scratch_shapes=[
+            pltpu.VMEM((rows, model), bf16),
+            pltpu.VMEM((1, model), f32),
             pltpu.VMEM((4, rows, half_width + 128), f32),
             pltpu.VMEM((n_wd, half_width, COLS), bf16),
             pltpu.VMEM((n_gu, model, COLS), bf16),
@@ -316,7 +392,7 @@
             pltpu.VMEM((rows, model), bf16),
             pltpu.VMEM((rows, units), bf16),
             pltpu.VMEM((n_wd, rows, COLS), f32),
-            dma((2 * n_wd,)), dma((2, n_gu)),
+            dma((2,)), dma((2 * n_wd,)), dma((2, n_gu)),
             dma((3,)), dma((3,)),
             dma((2, n_half)), dma((2, n_half)),
             dma((2, n_half)), dma((2, n_half)),
@@ -324,7 +400,7 @@
         ],
         compiler_params=pltpu.CompilerParams(collective_id=0, has_side_effects=True, vmem_limit_bytes=54 << 20),
         name="tail",
-    )(om, hidden, norm_mlp[None, :], w_out, w_gate_up, w_down)
+    )(pltpu.with_memory_space_constraint(om, pltpu.VMEM), *(pltpu.with_memory_space_constraint(x, pltpu.HBM) for x in (hidden, norm_mlp[None, :])), w_out, w_gate_up, w_down)
     return out.astype(bf16)
 
 
@@ -333,7 +409,9 @@
 
     def local_step(hidden, positions, norm_attn, norm_mlp, w_qkv, w_out, w_gate_up, w_down, k_cache, v_cache):
         num_rows, block_len, kv_local, head_dim = k_cache.shape
-        k_upd, v_upd, om = attend(positions, hidden, norm_attn, w_qkv, k_cache.transpose(0, 2, 3, 1), v_cache.transpose(0, 2, 3, 1))
+        k_t, v_t = k_cache.transpose(0, 2, 3, 1), v_cache.transpose(0, 2, 3, 1)
+        new_rows, k_ring, v_ring = project(positions, hidden, norm_attn, w_qkv, k_t, v_t)
+        k_upd, v_upd, om = attend(positions, new_rows, k_ring, v_ring, k_t, v_t)
         result = layer_tail(om, hidden, norm_mlp, w_out, w_gate_up, w_down, head_dim)
         return result, k_upd.transpose(0, 3, 1, 2), v_upd.transpose(0, 3, 1, 2)
 

time: 91.1 us -> 91.3 us (level)
  Pallas kernels: 87.4 us -> 90.1 us
  local copies, waits for them, and re-layouts: 1.34 us -> 0 us
  other arithmetic: 1.58 us -> 0.65 us
    pallas_call x1 -> x2, Pallas kernels: 27.3 us -> 49.7 us  [the longest x1 31.8 us: layer_tail(): pl.pallas_call(functools.partial(tail_kernel, dim), out_shape=pltpu.VMEM(...]
    pallas_call x1, Pallas kernels: 60 us -> 40.3 us  [attend(): pl.pallas_call(attend_kernel, out_shape=(jax.ShapeDtypeStruct(k_t.shape,...]
    another operation x1 -> x0, local copies, waits for them, and re-layouts: 1.34 us -> none
    convert_element_type x1, other arithmetic: 1.58 us -> 0.65 us  [layer_tail(): return out.astype(bf16)]
where the time goes in v4:
time: 91.3 us; the launch traced here: 91.4 us
  Pallas kernels  90.1 us (99%)
    pallas_call x1, Pallas kernels, attend(): pl.pallas_call(attend_kernel, out_shape=(jax.ShapeDtypeStruct(k_t.shape,...  40.3 us
    pallas_call x1, Pallas kernels, layer_tail(): pl.pallas_call(functools.partial(tail_kernel, dim), out_shape=pltpu.VMEM(...  31.8 us
    pallas_call x1, Pallas kernels, project(): pl.pallas_call(functools.partial(project_kernel, dim), out_shape=(pltpu.V...  17.9 us

profile of v4, /device:TPU:0, one launch (start us, length us, event | category | flops | bytes accessed | tf_op | source)
XLA Modules:
  0.0 91.4 jit_solution(15175894270658573188)
XLA Ops:
  0.6 17.9 %project.1 = (f32[4,16,1152]{2,1,0:T(8,128)S(1)}, bf16[7,16,96,768]{3,2,1,0:T(8,128)(2,1)S(1)}, bf16[7,16,96,768]{3,2,1,0:T(8,128)(2,1)S(1)}) custom-call(s32[16]{0:T(128)} %pos_hbm.3, bf16[16,3072]{1,0:T(8,128)(2,1)} %hid_hbm.3, f32[1,3072]{1,0:T(1,128)} %bitcast.10, bf16[3072,4608]{1,0:T(8,128)(2,1)} %w_hbm.1, bf16[16,16,96,768]{3,2,1,0:T(8,128)(2,1)} %bitcast.6, ...), custom_call_target="tpu_custom_call" | custom-call | tf_op jit(solution)/shard_map/project/pallas_call | solution.py:98
  18.6 40.3 %attend.1 = (bf16[16,16,96,768]{3,2,1,0:T(8,128)(2,1)}, bf16[16,16,96,768]{3,2,1,0:T(8,128)(2,1)}, f32[2,16,896]{2,1,0:T(8,128)S(1)}, bf16[7,16,96,768]{3,2,1,0:T(8,128)(2,1)S(1)}, bf16[7,16,96,768]{3,2,1,0:T(8,128)(2,1)S(1)}) custom-call(s32[16]{0:T(128)} %pos_hbm.3, ...), custom_call_target="tpu_custom_call", output_to_operand_aliasing={{3}: (2, {}), {4}: (3, {})} | custom-call | tf_op jit(solution)/shard_map/attend/pallas_call | solution.py:224
  58.9 31.8 %tail.1 = f32[16,3072]{1,0:T(8,128)S(1)} custom-call(f32[2,16,896]{2,1,0:T(8,128)S(1)} %get-tuple-element.12.om_ref, bf16[16,3072]{1,0:T(8,128)(2,1)} %hid_hbm.3, f32[1,3072]{1,0:T(1,128)} %bitcast.11, bf16[1536,3072]{1,0:T(8,128)(2,1)} %wo_hbm.1, bf16[3072,8192]{1,0:T(8,128)(2,1)} %wgu_hbm.1, bf16[4096,3072]{1,0:T(8,128)(2,1)} %wd_hbm.1), custom_call_target="tpu_custom_call" | custom-call | tf_op jit(solution)/shard_map/tail/pallas_call | solution.py:372
  90.7 0.7 convert_element_type.3

commit v5 on v4

--- a/solution.py
+++ b/solution.py
@@ -17,7 +17,7 @@
 
 QKV_COLS = 384
 SLOTS = 7
-PRE = 6
+PRE = 5
 
 
 def project_kernel(dim, pos_hbm, hid_hbm, gain_hbm, w_hbm, k_hbm, v_hbm, rows_ref, k_ring, v_ring,
@@ -36,7 +36,7 @@
     for b in range(PRE):
         loads.append(pltpu.make_async_copy(k_hbm.at[b], k_ring.at[b], in_sem.at[0, b]))
         loads.append(pltpu.make_async_copy(v_hbm.at[b], v_ring.at[b], in_sem.at[1, b]))
-    for copy in side + w_copies + loads:
+    for copy in side + w_copies:
         copy.start()
     barrier = pltpu.get_barrier_semaphore()
     for step in range(1, 4):
@@ -59,6 +59,8 @@
     pad = jnp.zeros((128 - rows, QKV_COLS), jnp.float32)
     for i in range(n_w):
         w_copies[i].wait()
+        for copy in loads[i * len(loads) // n_w:(i + 1) * len(loads) // n_w]:
+            copy.start()
         part = jnp.dot(normed_ref[...], w_buf[i], preferred_element_type=jnp.float32)
         qkv_t[i * QKV_COLS:(i + 1) * QKV_COLS, :] = jnp.concatenate([part, pad], axis=0).T
     third = mine // 3
@@ -270,7 +272,7 @@
     for i in range(n_wd):
         down_copies.append(pltpu.make_async_copy(wd_hbm.at[pl.ds(core * units, units), column(i)], wd.at[i], w_sem.at[n_wd + i]))
     side = [pltpu.make_async_copy(hid_hbm, hid_ref, side_sem.at[0]), pltpu.make_async_copy(gain_hbm, gain_ref, side_sem.at[1])]
-    for copy in weight_copies + side + gate_up_copies + down_copies:
+    for copy in side + weight_copies:
         copy.start()
 
     barrier = pltpu.get_barrier_semaphore()
@@ -292,8 +294,12 @@
         peer = lax.rem(sp + step, 4)
         o_copies.append(send(om_ref.at[lax.rem(peer, 2)], obuf.at[sp], o_send.at[step - 1], o_recv.at[step - 1], {'sp': peer}))
     obuf[sp] = om_ref[core]
+    for copy in gate_up_copies:
+        copy.start()
     for copy in o_copies:
         copy.wait_recv()
+    for copy in down_copies:
+        copy.start()
 
     heads = half_width // dim
     stats = [obuf[s, :, half_width:] for s in range(4)]

time: 91.3 us -> 79.6 us (0.87)
  Pallas kernels: 90.1 us -> 78.2 us
    pallas_call x1, Pallas kernels: 17.9 us -> 10.5 us  [project(): pl.pallas_call(functools.partial(project_kernel, dim), out_shape=(pltpu.V...]
    pallas_call x1, Pallas kernels: 31.8 us -> 25.8 us  [layer_tail(): pl.pallas_call(functools.partial(tail_kernel, dim), out_shape=pltpu.VMEM(...]
    pallas_call x1, Pallas kernels: 40.3 us -> 41.9 us  [attend(): pl.pallas_call(attend_kernel, out_shape=(jax.ShapeDtypeStruct(k_t.shape,...]
where the time goes in v5:
time: 79.6 us; the launch traced here: 79.5 us
  Pallas kernels  78.2 us (98%)
    pallas_call x1, Pallas kernels, attend(): pl.pallas_call(attend_kernel, out_shape=(jax.ShapeDtypeStruct(k_t.shape,...  41.9 us
    pallas_call x1, Pallas kernels, layer_tail(): pl.pallas_call(functools.partial(tail_kernel, dim), out_shape=pltpu.VMEM(...  25.8 us
    pallas_call x1, Pallas kernels, project(): pl.pallas_call(functools.partial(project_kernel, dim), out_shape=(pltpu.V...  10.5 us

profile of v5, /device:TPU:0, one launch (start us, length us, event | category | flops | bytes accessed | tf_op | source)
XLA Modules:
  0.0 79.5 jit_solution(905619360801344152)
XLA Ops:
  0.6 10.5 %project.1 = (f32[4,16,1152]{2,1,0:T(8,128)S(1)}, bf16[7,16,96,768]{3,2,1,0:T(8,128)(2,1)S(1)}, bf16[7,16,96,768]{3,2,1,0:T(8,128)(2,1)S(1)}) custom-call(s32[16]{0:T(128)} %pos_hbm.3, bf16[16,3072]{1,0:T(8,128)(2,1)} %hid_hbm.3, f32[1,3072]{1,0:T(1,128)} %bitcast.10, bf16[3072,4608]{1,0:T(8,128)(2,1)} %w_hbm.1, bf16[16,16,96,768]{3,2,1,0:T(8,128)(2,1)} %bitcast.6, ...), custom_call_target="tpu_custom_call" | custom-call | tf_op jit(solution)/shard_map/project/pallas_call | solution.py:100
  11.2 41.9 %attend.1 = (bf16[16,16,96,768]{3,2,1,0:T(8,128)(2,1)}, bf16[16,16,96,768]{3,2,1,0:T(8,128)(2,1)}, f32[2,16,896]{2,1,0:T(8,128)S(1)}, bf16[7,16,96,768]{3,2,1,0:T(8,128)(2,1)S(1)}, bf16[7,16,96,768]{3,2,1,0:T(8,128)(2,1)S(1)}) custom-call(s32[16]{0:T(128)} %pos_hbm.3, ...), custom_call_target="tpu_custom_call", output_to_operand_aliasing={{3}: (2, {}), {4}: (3, {})} | custom-call | tf_op jit(solution)/shard_map/attend/pallas_call | solution.py:226
  53.1 25.8 %tail.1 = f32[16,3072]{1,0:T(8,128)S(1)} custom-call(f32[2,16,896]{2,1,0:T(8,128)S(1)} %get-tuple-element.12.om_ref, bf16[16,3072]{1,0:T(8,128)(2,1)} %hid_hbm.3, f32[1,3072]{1,0:T(1,128)} %bitcast.11, bf16[1536,3072]{1,0:T(8,128)(2,1)} %wo_hbm.1, bf16[3072,8192]{1,0:T(8,128)(2,1)} %wgu_hbm.1, bf16[4096,3072]{1,0:T(8,128)(2,1)} %wd_hbm.1), custom_call_target="tpu_custom_call" | custom-call | tf_op jit(solution)/shard_map/tail/pallas_call | solution.py:378
  78.9 0.7 convert_element_type.3

commit v6 on v5

--- a/solution.py
+++ b/solution.py
@@ -16,8 +16,9 @@
 
 
 QKV_COLS = 384
-SLOTS = 7
+SLOTS = 8
 PRE = 5
+DRAIN = 3
 
 
 def project_kernel(dim, pos_hbm, hid_hbm, gain_hbm, w_hbm, k_hbm, v_hbm, rows_ref, k_ring, v_ring,
@@ -114,7 +115,7 @@
             pltpu.VMEM((4, rows, mine), f32),
             dma((mine // QKV_COLS,)), dma((2, PRE)), dma((3,)), dma((3,)), dma((3,)),
         ],
-        compiler_params=pltpu.CompilerParams(collective_id=1, has_side_effects=True, vmem_limit_bytes=14 << 20),
+        compiler_params=pltpu.CompilerParams(collective_id=1, has_side_effects=True, vmem_limit_bytes=9 << 20),
         name="project",
     )(*(pltpu.with_memory_space_constraint(x, pltpu.HBM) for x in (positions, hidden, norm_attn[None, :])), w_qkv, k_t, v_t)
 
@@ -171,11 +172,11 @@
         slot = lax.rem(b, SLOTS)
         pos = pos_ref[b]
 
-        @pl.when((b >= 2) & (b + SLOTS - 2 < rows))
+        @pl.when((b >= DRAIN) & (b + SLOTS - DRAIN < rows))
         def _():
             for which in range(2):
-                store(b - 2, which).wait()
-                load(b + SLOTS - 2, which).start()
+                store(b - DRAIN, which).wait()
+                load(b + SLOTS - DRAIN, which).start()
 
         @pl.when(b >= PRE)
         def _():
@@ -234,7 +235,7 @@
             dma((2, SLOTS)), dma((2, SLOTS)), dma,
         ],
         input_output_aliases={2: 3, 3: 4},
-        compiler_params=pltpu.CompilerParams(vmem_limit_bytes=10 << 20),
+        compiler_params=pltpu.CompilerParams(vmem_limit_bytes=6 << 20),
         name="attend",
     )(pltpu.with_memory_space_constraint(positions, pltpu.HBM), *(pltpu.with_memory_space_constraint(x, pltpu.VMEM) for x in (new_rows, k_ring, v_ring)), k_t, v_t)
     return k_upd, v_upd, om
@@ -244,41 +245,37 @@
 
 
 def tail_kernel(dim, om_ref, hid_hbm, gain_hbm, wo_hbm, wgu_hbm, wd_hbm, out_ref,
-                hid_ref, gain_ref, obuf, wo, wg, wu, wd, o_cat, snd, own, got, ysnd, ygot, x1, r2, act, x2,
-                side_sem, w_sem, gu_sem, o_send, o_recv, p_send, p_recv, y_send, y_recv, g_send, g_recv):
+                hid_ref, gain_ref, obuf, wo, wg, wu, wd, o_cat, o_snd, o_got, acc, ysnd, ygot, x1, r2, act, a_snd, a_got, x2,
+                side_sem, wo_sem, wd_sem, gu_sem, o_send, o_recv, p_send, p_recv, a_send, a_recv, y_send, y_recv, g_send, g_recv):
     tp, sp = lax.axis_index('tp'), lax.axis_index('sp')
     core = lax.rem(sp, 2)
     partner = sp + 1 - 2 * core
     rows = hid_ref.shape[0]
-    half_width = wo.shape[1]
+    half_width = wo.shape[2]
     n_half = x1.shape[0] // 2
-    n_gu, n_wd = wg.shape[0], wd.shape[0]
-    units = wd.shape[1]
+    n_gu = wg.shape[0]
+    units = wd.shape[2]
     ffn = wgu_hbm.shape[1] // 2
 
-    def column(index):
-        side = 1 - core if index < n_half else core
-        return pl.ds(pl.multiple_of((side * n_half + index % n_half) * COLS, COLS), COLS)
-
-    weight_copies = []
-    for i in range(n_wd):
-        weight_copies.append(pltpu.make_async_copy(wo_hbm.at[pl.ds(core * half_width, half_width), column(i)], wo.at[i], w_sem.at[i]))
-    gate_up_copies = []
+    def column(j):
+        return pl.ds(pl.multiple_of((core * n_half + j) * COLS, COLS), COLS)
+
+    side = [pltpu.make_async_copy(hid_hbm, hid_ref, side_sem.at[0]), pltpu.make_async_copy(gain_hbm, gain_ref, side_sem.at[1])]
+    out_copies, down_copies, gate_up_copies = [[], []], [[], []], []
+    for k, owner in enumerate((core, 1 - core)):
+        for j in range(n_half):
+            out_copies[k].append(pltpu.make_async_copy(wo_hbm.at[pl.ds(owner * half_width, half_width), column(j)], wo.at[k, j], wo_sem.at[k, j]))
+            down_copies[k].append(pltpu.make_async_copy(wd_hbm.at[pl.ds(owner * units, units), column(j)], wd.at[k, j], wd_sem.at[k, j]))
     for i in range(n_gu):
         first = core * units + i * COLS
         gate_up_copies.append(pltpu.make_async_copy(wgu_hbm.at[:, pl.ds(pl.multiple_of(first, COLS), COLS)], wg.at[i], gu_sem.at[0, i]))
         gate_up_copies.append(pltpu.make_async_copy(wgu_hbm.at[:, pl.ds(pl.multiple_of(ffn + first, COLS), COLS)], wu.at[i], gu_sem.at[1, i]))
-    down_copies = []
-    for i in range(n_wd):
-        down_copies.append(pltpu.make_async_copy(wd_hbm.at[pl.ds(core * units, units), column(i)], wd.at[i], w_sem.at[n_wd + i]))
-    side = [pltpu.make_async_copy(hid_hbm, hid_ref, side_sem.at[0]), pltpu.make_async_copy(gain_hbm, gain_ref, side_sem.at[1])]
-    for copy in side + weight_copies:
-        copy.start()
-
     barrier = pltpu.get_barrier_semaphore()
     for step in range(1, 4):
         pl.semaphore_signal(barrier, inc=1, device_id={'sp': lax.rem(sp + step, 4)}, device_id_type=MESH)
     pl.semaphore_signal(barrier, inc=1, device_id={'tp': 1 - tp}, device_id_type=MESH)
+    for copy in side + out_copies[0] + out_copies[1]:
+        copy.start()
     pl.semaphore_wait(barrier, 4)
 
     sent = []
@@ -289,16 +286,16 @@
         sent.append(copy)
         return copy
 
-    o_copies = []
+    first_copies = []
     for step in (2, 1, 3):
         peer = lax.rem(sp + step, 4)
-        o_copies.append(send(om_ref.at[lax.rem(peer, 2)], obuf.at[sp], o_send.at[step - 1], o_recv.at[step - 1], {'sp': peer}))
+        first_copies.append(send(om_ref.at[lax.rem(peer, 2)], obuf.at[sp], o_send.at[step - 1], o_recv.at[step - 1], {'sp': peer}))
     obuf[sp] = om_ref[core]
     for copy in gate_up_copies:
         copy.start()
-    for copy in o_copies:
+    for copy in first_copies:
         copy.wait_recv()
-    for copy in down_copies:
+    for copy in down_copies[0] + down_copies[1]:
         copy.start()
 
     heads = half_width // dim
@@ -317,22 +314,18 @@
                 scale = jnp.where(lane >= h * dim - 128 * k, betas[s][:, h:h + 1], scale)
             term = scale * obuf[s, :, 128 * k:128 * (k + 1)]
             value = term if value is None else value + term
-        o_cat[:, 128 * k:128 * (k + 1)] = value.astype(jnp.bfloat16)
-
-    def reduce_and_spread(stage, lhs_ref, w_ref, w_waits, base_of, dst):
-        lhs = lhs_ref[...]
-        first = []
-        for j in range(n_half):
-            w_waits[j].wait()
-            snd[stage, j] = jnp.dot(lhs, w_ref[j], preferred_element_type=jnp.float32)
-            first.append(send(snd.at[stage, j], got.at[stage, j], p_send.at[stage, j], p_recv.at[stage, j], {'sp': partner}))
-        for j in range(n_half):
-            w_waits[n_half + j].wait()
-            own[j] = jnp.dot(lhs, w_ref[n_half + j], preferred_element_type=jnp.float32)
+        value = value.astype(jnp.bfloat16)
+        o_cat[:, 128 * k:128 * (k + 1)] = value
+        o_snd[:, 128 * k:128 * (k + 1)] = value.astype(jnp.float32)
+
+    def product(lhs, w_ref, copies, j):
+        copies[j].wait()
+        return jnp.dot(lhs, w_ref[j], preferred_element_type=jnp.float32)
+
+    def spread(stage, part_of, base_of, dst):
         second = []
         for j in range(n_half):
-            first[j].wait_recv()
-            ysnd[stage, j] = (own[j] + got[stage, j]).astype(jnp.bfloat16).astype(jnp.float32)
+            ysnd[stage, j] = part_of(j).astype(jnp.bfloat16).astype(jnp.float32)
             second.append(send(ysnd.at[stage, j], ygot.at[stage, j], y_send.at[stage, j], y_recv.at[stage, j], {'tp': 1 - tp}))
         third = []
         for j in range(n_half):
@@ -342,9 +335,14 @@
         for copy in third:
             copy.wait_recv()
 
+    o_copy = send(o_snd, o_got, p_send, p_recv, {'sp': partner})
+    for j in range(n_half):
+        acc[j] = product(o_cat[...], wo.at[0], out_copies[0], j)
     for copy in side:
         copy.wait()
-    reduce_and_spread(0, o_cat, wo, weight_copies, lambda j: hid_ref[:, column(n_half + j)].astype(jnp.float32), x1)
+    o_copy.wait_recv()
+    o_other = o_got[...].astype(jnp.bfloat16)
+    spread(0, lambda j: acc[j] + product(o_other, wo.at[1], out_copies[1], j), lambda j: hid_ref[:, column(j)].astype(jnp.float32), x1)
 
     square = functools.reduce(lambda a, b: a + b, [x1[i] * x1[i] for i in range(2 * n_half)])
     inv = lax.rsqrt(jnp.sum(square, axis=1, keepdims=True) / (2 * n_half * COLS) + NORM_EPS)
@@ -352,14 +350,22 @@
         cut = slice(i * COLS, (i + 1) * COLS)
         r2[:, cut] = (x1[i] * inv * gain_ref[:, cut]).astype(jnp.bfloat16)
 
+    a_copies = []
     for i in range(n_gu):
         gate_up_copies[2 * i].wait()
         gate_up_copies[2 * i + 1].wait()
         gate = jnp.dot(r2[...], wg[i], preferred_element_type=jnp.float32)
         up = jnp.dot(r2[...], wu[i], preferred_element_type=jnp.float32)
-        act[:, i * COLS:(i + 1) * COLS] = (gate * jax.nn.sigmoid(gate) * up).astype(jnp.bfloat16)
-
-    reduce_and_spread(1, act, wd, down_copies, lambda j: x1[core * n_half + j], x2)
+        value = (gate * jax.nn.sigmoid(gate) * up).astype(jnp.bfloat16)
+        act[0, :, i * COLS:(i + 1) * COLS] = value
+        a_snd[i] = value.astype(jnp.float32)
+        a_copies.append(send(a_snd.at[i], a_got.at[i], a_send.at[i], a_recv.at[i], {'sp': partner}))
+    for j in range(n_half):
+        acc[j] = product(act[0], wd.at[0], down_copies[0], j)
+    for i in range(n_gu):
+        a_copies[i].wait_recv()
+        act[1, :, i * COLS:(i + 1) * COLS] = a_got[i].astype(jnp.bfloat16)
+    spread(1, lambda j: acc[j] + product(act[1], wd.at[1], down_copies[1], j), lambda j: x1[core * n_half + j], x2)
     for i in range(2 * n_half):
         out_ref[:, i * COLS:(i + 1) * COLS] = x2[i]
     for copy in sent:
@@ -384,23 +390,26 @@
             pltpu.VMEM((rows, model), bf16),
             pltpu.VMEM((1, model), f32),
             pltpu.VMEM((4, rows, half_width + 128), f32),
-            pltpu.VMEM((n_wd, half_width, COLS), bf16),
+            pltpu.VMEM((2, n_half, half_width, COLS), bf16),
             pltpu.VMEM((n_gu, model, COLS), bf16),
             pltpu.VMEM((n_gu, model, COLS), bf16),
-            pltpu.VMEM((n_wd, units, COLS), bf16),
+            pltpu.VMEM((2, n_half, units, COLS), bf16),
             pltpu.VMEM((rows, half_width), bf16),
-            pltpu.VMEM((2, n_half, rows, COLS), f32),
+            pltpu.VMEM((rows, half_width), f32),
+            pltpu.VMEM((rows, half_width), f32),
             pltpu.VMEM((n_half, rows, COLS), f32),
-            pltpu.VMEM((2, n_half, rows, COLS), f32),
             pltpu.VMEM((2, n_half, rows, COLS), f32),
             pltpu.VMEM((2, n_half, rows, COLS), f32),
             pltpu.VMEM((n_wd, rows, COLS), f32),
             pltpu.VMEM((rows, model), bf16),
-            pltpu.VMEM((rows, units), bf16),
+            pltpu.VMEM((2, rows, units), bf16),
+            pltpu.VMEM((n_gu, rows, COLS), f32),
+            pltpu.VMEM((n_gu, rows, COLS), f32),
             pltpu.VMEM((n_wd, rows, COLS), f32),
-            dma((2,)), dma((2 * n_wd,)), dma((2, n_gu)),
+            dma((2,)), dma((2, n_half)), dma((2, n_half)), dma((2, n_gu)),
             dma((3,)), dma((3,)),
-            dma((2, n_half)), dma((2, n_half)),
+            dma, dma,
+            dma((n_gu,)), dma((n_gu,)),
             dma((2, n_half)), dma((2, n_half)),
             dma((2, n_half)), dma((2, n_half)),
         ],

time: 79.6 us -> 78.7 us (0.989)
  Pallas kernels: 78.2 us -> 77.4 us
    pallas_call x1, Pallas kernels: 25.8 us -> 24.9 us  [layer_tail(): pl.pallas_call(functools.partial(tail_kernel, dim), out_shape=pltpu.VMEM(...]
where the time goes in v6:
time: 78.7 us
  Pallas kernels  77.4 us (98%)
    pallas_call x1, Pallas kernels, attend(): pl.pallas_call(attend_kernel, out_shape=(jax.ShapeDtypeStruct(k_t.shape,...  41.9 us
    pallas_call x1, Pallas kernels, layer_tail(): pl.pallas_call(functools.partial(tail_kernel, dim), out_shape=pltpu.VMEM(...  24.9 us
    pallas_call x1, Pallas kernels, project(): pl.pallas_call(functools.partial(project_kernel, dim), out_shape=(pltpu.V...  10.5 us

profile of v6, /device:TPU:0, one launch (start us, length us, event | category | flops | bytes accessed | tf_op | source)
XLA Modules:
  0.0 78.7 jit_solution(13509657533612848475)
XLA Ops:
  0.6 10.5 %project.1 = (f32[4,16,1152]{2,1,0:T(8,128)S(1)}, bf16[8,16,96,768]{3,2,1,0:T(8,128)(2,1)S(1)}, bf16[8,16,96,768]{3,2,1,0:T(8,128)(2,1)S(1)}) custom-call(s32[16]{0:T(128)} %pos_hbm.3, bf16[16,3072]{1,0:T(8,128)(2,1)} %hid_hbm.3, f32[1,3072]{1,0:T(1,128)} %bitcast.10, bf16[3072,4608]{1,0:T(8,128)(2,1)} %w_hbm.1, bf16[16,16,96,768]{3,2,1,0:T(8,128)(2,1)} %bitcast.6, ...), custom_call_target="tpu_custom_call" | custom-call | tf_op jit(solution)/shard_map/project/pallas_call | solution.py:101
  11.2 41.9 %attend.1 = (bf16[16,16,96,768]{3,2,1,0:T(8,128)(2,1)}, bf16[16,16,96,768]{3,2,1,0:T(8,128)(2,1)}, f32[2,16,896]{2,1,0:T(8,128)S(1)}, bf16[8,16,96,768]{3,2,1,0:T(8,128)(2,1)S(1)}, bf16[8,16,96,768]{3,2,1,0:T(8,128)(2,1)S(1)}) custom-call(s32[16]{0:T(128)} %pos_hbm.3, ...), custom_call_target="tpu_custom_call", output_to_operand_aliasing={{3}: (2, {}), {4}: (3, {})} | custom-call | tf_op jit(solution)/shard_map/attend/pallas_call | solution.py:227
  53.1 24.9 %tail.1 = f32[16,3072]{1,0:T(8,128)S(1)} custom-call(f32[2,16,896]{2,1,0:T(8,128)S(1)} %get-tuple-element.12.om_ref, bf16[16,3072]{1,0:T(8,128)(2,1)} %hid_hbm.3, f32[1,3072]{1,0:T(1,128)} %bitcast.11, bf16[1536,3072]{1,0:T(8,128)(2,1)} %wo_hbm.1, bf16[3072,8192]{1,0:T(8,128)(2,1)} %wgu_hbm.1, bf16[4096,3072]{1,0:T(8,128)(2,1)} %wd_hbm.1), custom_call_target="tpu_custom_call" | custom-call | tf_op jit(solution)/shard_map/tail/pallas_call | solution.py:384
  78.0 0.7 convert_element_type.3

commit v7 on v6

--- a/solution.py
+++ b/solution.py
@@ -17,11 +17,11 @@
 
 QKV_COLS = 384
 SLOTS = 8
-PRE = 5
+PRE = 7
 DRAIN = 3
 
 
-def project_kernel(dim, pos_hbm, hid_hbm, gain_hbm, w_hbm, k_hbm, v_hbm, rows_ref, k_ring, v_ring,
+def project_kernel(dim, pos_hbm, hid_hbm, gain_hbm, w_hbm, k_hbm, v_hbm, q_ref, new_t, k_ring, v_ring,
                    pos_ref, hid_ref, gain_ref, w_buf, normed_ref, qkv_t, turned, msg, gath,
                    w_sem, in_sem, side_sem, s_send, s_recv):
     sp = lax.axis_index('sp')
@@ -85,7 +85,12 @@
     gath[sp] = own_rows
     for copy in sends:
         copy.wait_recv()
-    rows_ref[...] = gath[...]
+    q_ref[...] = gath[:, :, :third]
+    pad = jnp.zeros((128 - rows, third), jnp.float32)
+    for which in range(2):
+        for s in range(4):
+            entry = gath[s, :, (1 + which) * third:(2 + which) * third]
+            new_t[which, s * third:(s + 1) * third, :] = jnp.concatenate([entry, pad], axis=0).T
     for copy in loads:
         copy.wait()
     for copy in sends:
@@ -100,9 +105,9 @@
     f32, bf16, dma = jnp.float32, jnp.bfloat16, pltpu.SemaphoreType.DMA
     return pl.pallas_call(
         functools.partial(project_kernel, dim),
-        out_shape=(pltpu.VMEM((4, rows, mine), f32), pltpu.VMEM((SLOTS, heads, dim, block), bf16), pltpu.VMEM((SLOTS, heads, dim, block), bf16)),
+        out_shape=(pltpu.VMEM((4, rows, mine // 3), f32), pltpu.VMEM((2, heads * dim, 128), f32), pltpu.VMEM((SLOTS, heads, dim, block), bf16), pltpu.VMEM((SLOTS, heads, dim, block), bf16)),
         in_specs=[hbm] * 6,
-        out_specs=(vmem, vmem, vmem),
+        out_specs=(vmem, vmem, vmem, vmem),
         scratch_shapes=[
             pltpu.SMEM((rows,), jnp.int32),
             pltpu.VMEM((rows, model), bf16),
@@ -115,16 +120,16 @@
             pltpu.VMEM((4, rows, mine), f32),
             dma((mine // QKV_COLS,)), dma((2, PRE)), dma((3,)), dma((3,)), dma((3,)),
         ],
-        compiler_params=pltpu.CompilerParams(collective_id=1, has_side_effects=True, vmem_limit_bytes=9 << 20),
+        compiler_params=pltpu.CompilerParams(collective_id=1, has_side_effects=True, vmem_limit_bytes=8200 << 10),
         name="project",
     )(*(pltpu.with_memory_space_constraint(x, pltpu.HBM) for x in (positions, hidden, norm_attn[None, :])), w_qkv, k_t, v_t)
 
 
-def attend_kernel(pos_hbm, rows_ref, k_in, v_in, k_hbm, v_hbm, ko_hbm, vo_hbm, om_ref, k_ring, v_ring,
-                  pos_ref, new_t, in_sem, out_sem, side_sem):
-    rows = rows_ref.shape[1]
+def attend_kernel(pos_hbm, q_ref, new_t, k_in, v_in, k_hbm, v_hbm, ko_hbm, vo_hbm, om_ref, k_ring, v_ring,
+                  pos_ref, in_sem, out_sem, side_sem):
+    rows, third = q_ref.shape[1:]
     heads, dim, block = k_ring.shape[1:]
-    width, third = heads * dim, rows_ref.shape[2] // 3
+    width = heads * dim
     base = lax.axis_index('sp') * block
 
     def load(b, which):
@@ -142,11 +147,6 @@
     for b in range(PRE, SLOTS):
         load(b, 0).start()
         load(b, 1).start()
-    pad = jnp.zeros((128 - rows, third), jnp.float32)
-    for which in range(2):
-        for s in range(4):
-            entry = rows_ref[s, :, (1 + which) * third:(2 + which) * third]
-            new_t[which, s * third:(s + 1) * third, :] = jnp.concatenate([entry, pad], axis=0).T
     pos_copy.wait()
 
     own = lax.broadcasted_iota(jnp.int32, (heads, width), 1) // dim == lax.broadcasted_iota(jnp.int32, (heads, width), 0)
@@ -184,7 +184,7 @@
 
         patch(k_ring, slot, 0, b, pos)
         store(b, 0).start()
-        q_row = jnp.concatenate([rows_ref[s, pl.ds(b, 1), :third] for s in range(4)], axis=1)
+        q_row = jnp.concatenate([q_ref[s, pl.ds(b, 1), :] for s in range(4)], axis=1)
         q_diag = jnp.where(own, jnp.broadcast_to(q_row, (heads, width)), 0.0).astype(jnp.bfloat16)
         scores = jnp.dot(q_diag, k_ring[slot].reshape(width, block), preferred_element_type=jnp.float32) * (dim ** -0.5)
         slot_ids = lax.broadcasted_iota(jnp.int32, (heads, block), 1) + base
@@ -217,7 +217,7 @@
         store(b, 1).wait()
 
 
-def attend(positions, new_rows, k_ring, v_ring, k_t, v_t):
+def attend(positions, q_rows, new_t, k_ring, v_ring, k_t, v_t):
     rows, heads, dim, block = k_t.shape
     width = heads * dim
     vmem = pl.BlockSpec(memory_space=pltpu.VMEM)
@@ -227,17 +227,16 @@
     k_upd, v_upd, om, _, _ = pl.pallas_call(
         attend_kernel,
         out_shape=(jax.ShapeDtypeStruct(k_t.shape, k_t.dtype), jax.ShapeDtypeStruct(v_t.shape, v_t.dtype), pltpu.VMEM((2, rows, width // 2 + 128), f32), ring, ring),
-        in_specs=[hbm, vmem, vmem, vmem, hbm, hbm],
+        in_specs=[hbm, vmem, vmem, vmem, vmem, hbm, hbm],
         out_specs=(hbm, hbm, vmem, vmem, vmem),
         scratch_shapes=[
             pltpu.SMEM((rows,), jnp.int32),
-            pltpu.VMEM((2, width, 128), f32),
             dma((2, SLOTS)), dma((2, SLOTS)), dma,
         ],
-        input_output_aliases={2: 3, 3: 4},
-        compiler_params=pltpu.CompilerParams(vmem_limit_bytes=6 << 20),
+        input_output_aliases={3: 3, 4: 4},
+        compiler_params=pltpu.CompilerParams(vmem_limit_bytes=5 << 20),
         name="attend",
-    )(pltpu.with_memory_space_constraint(positions, pltpu.HBM), *(pltpu.with_memory_space_constraint(x, pltpu.VMEM) for x in (new_rows, k_ring, v_ring)), k_t, v_t)
+    )(pltpu.with_memory_space_constraint(positions, pltpu.HBM), *(pltpu.with_memory_space_constraint(x, pltpu.VMEM) for x in (q_rows, new_t, k_ring, v_ring)), k_t, v_t)
     return k_upd, v_upd, om
 
 
@@ -425,8 +424,8 @@
     def local_step(hidden, positions, norm_attn, norm_mlp, w_qkv, w_out, w_gate_up, w_down, k_cache, v_cache):
         num_rows, block_len, kv_local, head_dim = k_cache.shape
         k_t, v_t = k_cache.transpose(0, 2, 3, 1), v_cache.transpose(0, 2, 3, 1)
-        new_rows, k_ring, v_ring = project(positions, hidden, norm_attn, w_qkv, k_t, v_t)
-        k_upd, v_upd, om = attend(positions, new_rows, k_ring, v_ring, k_t, v_t)
+        q_rows, new_t, k_ring, v_ring = project(positions, hidden, norm_attn, w_qkv, k_t, v_t)
+        k_upd, v_upd, om = attend(positions, q_rows, new_t, k_ring, v_ring, k_t, v_t)
         result = layer_tail(om, hidden, norm_mlp, w_out, w_gate_up, w_down, head_dim)
         return result, k_upd.transpose(0, 3, 1, 2), v_upd.transpose(0, 3, 1, 2)
 

time: 78.7 us -> 78.4 us (level)
    pallas_call x1, Pallas kernels: 41.9 us -> 38.9 us  [attend(): pl.pallas_call(attend_kernel, out_shape=(jax.ShapeDtypeStruct(k_t.shape,...]
    pallas_call x1, Pallas kernels: 10.5 us -> 13 us  [project(): pl.pallas_call(functools.partial(project_kernel, dim), out_shape=(pltpu.V...]
where the time goes in v7:
time: 78.4 us; the launch traced here: 78.1 us
  Pallas kernels  76.8 us (98%)
    pallas_call x1, Pallas kernels, attend(): pl.pallas_call(attend_kernel, out_shape=(jax.ShapeDtypeStruct(k_t.shape,...  38.9 us
    pallas_call x1, Pallas kernels, layer_tail(): pl.pallas_call(functools.partial(tail_kernel, dim), out_shape=pltpu.VMEM(...  24.9 us
    pallas_call x1, Pallas kernels, project(): pl.pallas_call(functools.partial(project_kernel, dim), out_shape=(pltpu.V...  13 us

profile of v7, /device:TPU:0, one launch (start us, length us, event | category | flops | bytes accessed | tf_op | source)
XLA Modules:
  0.0 78.1 jit_solution(16390884116263324478)
XLA Ops:
  0.6 13.0 %project.1 = (f32[4,16,384]{2,1,0:T(8,128)S(1)}, f32[2,1536,128]{2,1,0:T(8,128)S(1)}, bf16[8,16,96,768]{3,2,1,0:T(8,128)(2,1)S(1)}, bf16[8,16,96,768]{3,2,1,0:T(8,128)(2,1)S(1)}) custom-call(s32[16]{0:T(128)} %pos_hbm.3, bf16[16,3072]{1,0:T(8,128)(2,1)} %hid_hbm.3, f32[1,3072]{1,0:T(1,128)} %bitcast.10, bf16[3072,4608]{1,0:T(8,128)(2,1)} %w_hbm.1, ...), custom_call_target="tpu_custom_call" | custom-call | tf_op jit(solution)/shard_map/project/pallas_call | solution.py:106
  13.7 38.9 %attend.1 = (bf16[16,16,96,768]{3,2,1,0:T(8,128)(2,1)}, bf16[16,16,96,768]{3,2,1,0:T(8,128)(2,1)}, f32[2,16,896]{2,1,0:T(8,128)S(1)}, bf16[8,16,96,768]{3,2,1,0:T(8,128)(2,1)S(1)}, bf16[8,16,96,768]{3,2,1,0:T(8,128)(2,1)S(1)}) custom-call(s32[16]{0:T(128)} %pos_hbm.3, ...), custom_call_target="tpu_custom_call", output_to_operand_aliasing={{3}: (3, {}), {4}: (4, {})} | custom-call | tf_op jit(solution)/shard_map/attend/pallas_call | solution.py:227
  52.6 24.9 %tail.1 = f32[16,3072]{1,0:T(8,128)S(1)} custom-call(f32[2,16,896]{2,1,0:T(8,128)S(1)} %get-tuple-element.14.om_ref, bf16[16,3072]{1,0:T(8,128)(2,1)} %hid_hbm.3, f32[1,3072]{1,0:T(1,128)} %bitcast.11, bf16[1536,3072]{1,0:T(8,128)(2,1)} %wo_hbm.1, bf16[3072,8192]{1,0:T(8,128)(2,1)} %wgu_hbm.1, bf16[4096,3072]{1,0:T(8,128)(2,1)} %wd_hbm.1), custom_call_target="tpu_custom_call" | custom-call | tf_op jit(solution)/shard_map/tail/pallas_call | solution.py:383
  77.4 0.7 convert_element_type.3

commit v8 on v7

--- a/solution.py
+++ b/solution.py
@@ -37,7 +37,7 @@
     for b in range(PRE):
         loads.append(pltpu.make_async_copy(k_hbm.at[b], k_ring.at[b], in_sem.at[0, b]))
         loads.append(pltpu.make_async_copy(v_hbm.at[b], v_ring.at[b], in_sem.at[1, b]))
-    for copy in side + w_copies:
+    for copy in side + w_copies + loads[:2]:
         copy.start()
     barrier = pltpu.get_barrier_semaphore()
     for step in range(1, 4):
@@ -60,7 +60,7 @@
     pad = jnp.zeros((128 - rows, QKV_COLS), jnp.float32)
     for i in range(n_w):
         w_copies[i].wait()
-        for copy in loads[i * len(loads) // n_w:(i + 1) * len(loads) // n_w]:
+        for copy in loads[2 + 4 * i:6 + 4 * i]:
             copy.start()
         part = jnp.dot(normed_ref[...], w_buf[i], preferred_element_type=jnp.float32)
         qkv_t[i * QKV_COLS:(i + 1) * QKV_COLS, :] = jnp.concatenate([part, pad], axis=0).T
@@ -183,7 +183,7 @@
             load(b, 0).wait()
 
         patch(k_ring, slot, 0, b, pos)
-        store(b, 0).start()
+        store(b, 0).start(priority=1)
         q_row = jnp.concatenate([q_ref[s, pl.ds(b, 1), :] for s in range(4)], axis=1)
         q_diag = jnp.where(own, jnp.broadcast_to(q_row, (heads, width)), 0.0).astype(jnp.bfloat16)
         scores = jnp.dot(q_diag, k_ring[slot].reshape(width, block), preferred_element_type=jnp.float32) * (dim ** -0.5)
@@ -199,7 +199,7 @@
             load(b, 1).wait()
 
         patch(v_ring, slot, 1, b, pos)
-        store(b, 1).start()
+        store(b, 1).start(priority=1)
         acc = lax.dot_general(weights.astype(jnp.bfloat16), v_ring[slot].reshape(width, block), (((1,), (1,)), ((), ())), preferred_element_type=jnp.float32)
         o_row = jnp.sum(jnp.where(own, acc, 0.0), axis=0, keepdims=True)
         for core in range(2):

time: 78.4 us -> 78.2 us (level)
  no operation moved by 1% of the time
where the time goes in v8:
time: 78.2 us
  Pallas kernels  76.9 us (98%)
    pallas_call x1, Pallas kernels, attend(): pl.pallas_call(attend_kernel, out_shape=(jax.ShapeDtypeStruct(k_t.shape,...  38.8 us
    pallas_call x1, Pallas kernels, layer_tail(): pl.pallas_call(functools.partial(tail_kernel, dim), out_shape=pltpu.VMEM(...  25.1 us
    pallas_call x1, Pallas kernels, project(): pl.pallas_call(functools.partial(project_kernel, dim), out_shape=(pltpu.V...  13 us

profile of v8, /device:TPU:0, one launch (start us, length us, event | category | flops | bytes accessed | tf_op | source)
XLA Modules:
  0.0 78.2 jit_solution(7227108188641239597)
XLA Ops:
  0.6 13.0 %project.1 = (f32[4,16,384]{2,1,0:T(8,128)S(1)}, f32[2,1536,128]{2,1,0:T(8,128)S(1)}, bf16[8,16,96,768]{3,2,1,0:T(8,128)(2,1)S(1)}, bf16[8,16,96,768]{3,2,1,0:T(8,128)(2,1)S(1)}) custom-call(s32[16]{0:T(128)} %pos_hbm.3, bf16[16,3072]{1,0:T(8,128)(2,1)} %hid_hbm.3, f32[1,3072]{1,0:T(1,128)} %bitcast.10, bf16[3072,4608]{1,0:T(8,128)(2,1)} %w_hbm.1, ...), custom_call_target="tpu_custom_call" | custom-call | tf_op jit(solution)/shard_map/project/pallas_call | solution.py:106
  13.7 38.8 %attend.1 = (bf16[16,16,96,768]{3,2,1,0:T(8,128)(2,1)}, bf16[16,16,96,768]{3,2,1,0:T(8,128)(2,1)}, f32[2,16,896]{2,1,0:T(8,128)S(1)}, bf16[8,16,96,768]{3,2,1,0:T(8,128)(2,1)S(1)}, bf16[8,16,96,768]{3,2,1,0:T(8,128)(2,1)S(1)}) custom-call(s32[16]{0:T(128)} %pos_hbm.3, ...), custom_call_target="tpu_custom_call", output_to_operand_aliasing={{3}: (3, {}), {4}: (4, {})} | custom-call | tf_op jit(solution)/shard_map/attend/pallas_call | solution.py:227
  52.5 25.1 %tail.1 = f32[16,3072]{1,0:T(8,128)S(1)} custom-call(f32[2,16,896]{2,1,0:T(8,128)S(1)} %get-tuple-element.14.om_ref, bf16[16,3072]{1,0:T(8,128)(2,1)} %hid_hbm.3, f32[1,3072]{1,0:T(1,128)} %bitcast.11, bf16[1536,3072]{1,0:T(8,128)(2,1)} %wo_hbm.1, bf16[3072,8192]{1,0:T(8,128)(2,1)} %wgu_hbm.1, bf16[4096,3072]{1,0:T(8,128)(2,1)} %wd_hbm.1), custom_call_target="tpu_custom_call" | custom-call | tf_op jit(solution)/shard_map/tail/pallas_call | solution.py:383
  77.5 0.7 convert_element_type.3

commit v9 on v7

--- a/solution.py
+++ b/solution.py
@@ -19,6 +19,7 @@
 SLOTS = 8
 PRE = 7
 DRAIN = 3
+LEFT = 4
 
 
 def project_kernel(dim, pos_hbm, hid_hbm, gain_hbm, w_hbm, k_hbm, v_hbm, q_ref, new_t, k_ring, v_ring,
@@ -125,12 +126,13 @@
     )(*(pltpu.with_memory_space_constraint(x, pltpu.HBM) for x in (positions, hidden, norm_attn[None, :])), w_qkv, k_t, v_t)
 
 
-def attend_kernel(pos_hbm, q_ref, new_t, k_in, v_in, k_hbm, v_hbm, ko_hbm, vo_hbm, om_ref, k_ring, v_ring,
+def attend_kernel(pos_hbm, q_ref, new_t, k_in, v_in, k_hbm, v_hbm, ko_hbm, vo_hbm, own_ref, other_ref, k_ring, v_ring,
                   pos_ref, in_sem, out_sem, side_sem):
     rows, third = q_ref.shape[1:]
     heads, dim, block = k_ring.shape[1:]
     width = heads * dim
     base = lax.axis_index('sp') * block
+    core = lax.rem(lax.axis_index('sp'), 2)
 
     def load(b, which):
         slot = lax.rem(b, SLOTS)
@@ -183,7 +185,7 @@
             load(b, 0).wait()
 
         patch(k_ring, slot, 0, b, pos)
-        store(b, 0).start()
+        pl.when(b < rows - LEFT)(lambda: store(b, 0).start())
         q_row = jnp.concatenate([q_ref[s, pl.ds(b, 1), :] for s in range(4)], axis=1)
         q_diag = jnp.where(own, jnp.broadcast_to(q_row, (heads, width)), 0.0).astype(jnp.bfloat16)
         scores = jnp.dot(q_diag, k_ring[slot].reshape(width, block), preferred_element_type=jnp.float32) * (dim ** -0.5)
@@ -199,20 +201,22 @@
             load(b, 1).wait()
 
         patch(v_ring, slot, 1, b, pos)
-        store(b, 1).start()
+        pl.when(b < rows - LEFT)(lambda: store(b, 1).start())
         acc = lax.dot_general(weights.astype(jnp.bfloat16), v_ring[slot].reshape(width, block), (((1,), (1,)), ((), ())), preferred_element_type=jnp.float32)
         o_row = jnp.sum(jnp.where(own, acc, 0.0), axis=0, keepdims=True)
-        for core in range(2):
-            local = head_ids - core * half_heads
+        pieces = []
+        for half in range(2):
+            local = head_ids - half * half_heads
             keep = (local >= 0) & (local < half_heads)
             stats = jnp.where(keep & (lane_ids == local), row_max, 0.0) + jnp.where(keep & (lane_ids == local + half_heads), row_sum, 0.0)
-            row = jnp.concatenate([o_row[:, core * half_width:(core + 1) * half_width], jnp.sum(stats, axis=0, keepdims=True)], axis=1)
-            at_row = lax.broadcasted_iota(jnp.int32, (rows, half_width + 128), 0) == b
-            om_ref[core] = jnp.where(at_row, row, om_ref[core])
+            pieces.append(jnp.concatenate([o_row[:, half * half_width:(half + 1) * half_width], jnp.sum(stats, axis=0, keepdims=True)], axis=1))
+        at_row = lax.broadcasted_iota(jnp.int32, (rows, half_width + 128), 0) == b
+        own_ref[...] = jnp.where(at_row, jnp.where(core == 0, pieces[0], pieces[1]), own_ref[...])
+        other_ref[...] = jnp.where(at_row, jnp.where(core == 0, pieces[1], pieces[0]), other_ref[...])
         return carry
 
     lax.fori_loop(0, rows, step, 0)
-    for b in range(rows - SLOTS, rows):
+    for b in range(rows - SLOTS, rows - LEFT):
         store(b, 0).wait()
         store(b, 1).wait()
 
@@ -224,28 +228,56 @@
     hbm = pl.BlockSpec(memory_space=pl.ANY)
     f32, bf16, dma = jnp.float32, jnp.bfloat16, pltpu.SemaphoreType.DMA
     ring = pltpu.VMEM((SLOTS, heads, dim, block), bf16)
-    k_upd, v_upd, om, _, _ = pl.pallas_call(
+    part = jax.ShapeDtypeStruct((rows, width // 2 + 128), f32)
+    return pl.pallas_call(
         attend_kernel,
-        out_shape=(jax.ShapeDtypeStruct(k_t.shape, k_t.dtype), jax.ShapeDtypeStruct(v_t.shape, v_t.dtype), pltpu.VMEM((2, rows, width // 2 + 128), f32), ring, ring),
+        out_shape=(jax.ShapeDtypeStruct(k_t.shape, k_t.dtype), jax.ShapeDtypeStruct(v_t.shape, v_t.dtype), part, part, ring, ring),
         in_specs=[hbm, vmem, vmem, vmem, vmem, hbm, hbm],
-        out_specs=(hbm, hbm, vmem, vmem, vmem),
+        out_specs=(hbm, hbm, vmem, vmem, vmem, vmem),
         scratch_shapes=[
             pltpu.SMEM((rows,), jnp.int32),
             dma((2, SLOTS)), dma((2, SLOTS)), dma,
         ],
-        input_output_aliases={3: 3, 4: 4},
+        input_output_aliases={3: 4, 4: 5},
         compiler_params=pltpu.CompilerParams(vmem_limit_bytes=5 << 20),
         name="attend",
     )(pltpu.with_memory_space_constraint(positions, pltpu.HBM), *(pltpu.with_memory_space_constraint(x, pltpu.VMEM) for x in (q_rows, new_t, k_ring, v_ring)), k_t, v_t)
-    return k_upd, v_upd, om
+
+
+def write_kernel(k_ring, v_ring, k_in, v_in, ko_hbm, vo_hbm, sem):
+    rows = ko_hbm.shape[0]
+    copies = []
+    for b in range(rows - LEFT, rows):
+        for which, (ring, dst) in enumerate(((k_ring, ko_hbm), (v_ring, vo_hbm))):
+            copies.append(pltpu.make_async_copy(ring.at[b % SLOTS], dst.at[b], sem.at[which, b - rows + LEFT]))
+    for copy in copies:
+        copy.start()
+    for copy in copies:
+        copy.wait()
+
+
+def write_rest(k_ring, v_ring, k_upd, v_upd):
+    vmem = pl.BlockSpec(memory_space=pltpu.VMEM)
+    hbm = pl.BlockSpec(memory_space=pl.ANY)
+    return pl.pallas_call(
+        write_kernel,
+        out_shape=(jax.ShapeDtypeStruct(k_upd.shape, k_upd.dtype), jax.ShapeDtypeStruct(v_upd.shape, v_upd.dtype)),
+        in_specs=[vmem, vmem, hbm, hbm],
+        out_specs=(hbm, hbm),
+        scratch_shapes=[pltpu.SemaphoreType.DMA((2, LEFT))],
+        input_output_aliases={2: 0, 3: 1},
+        cost_estimate=pl.CostEstimate(flops=10 ** 10, bytes_accessed=19 << 20, transcendentals=0),
+        compiler_params=pltpu.CompilerParams(vmem_limit_bytes=1 << 20),
+        name="write_rest",
+    )(*(pltpu.with_memory_space_constraint(x, pltpu.VMEM) for x in (k_ring, v_ring)), k_upd, v_upd)
 
 
 COLS = 512
 
 
-def tail_kernel(dim, om_ref, hid_hbm, gain_hbm, wo_hbm, wgu_hbm, wd_hbm, out_ref,
+def tail_kernel(dim, own_ref, in1_ref, in2_ref, in3_ref, hid_hbm, gain_hbm, wo_hbm, wgu_hbm, wd_hbm, out_ref,
                 hid_ref, gain_ref, obuf, wo, wg, wu, wd, o_cat, o_snd, o_got, acc, ysnd, ygot, x1, r2, act, a_snd, a_got, x2,
-                side_sem, wo_sem, wd_sem, gu_sem, o_send, o_recv, p_send, p_recv, a_send, a_recv, y_send, y_recv, g_send, g_recv):
+                side_sem, wo_sem, wd_sem, gu_sem, p_send, p_recv, a_send, a_recv, y_send, y_recv, g_send, g_recv):
     tp, sp = lax.axis_index('tp'), lax.axis_index('sp')
     core = lax.rem(sp, 2)
     partner = sp + 1 - 2 * core
@@ -270,12 +302,10 @@
         gate_up_copies.append(pltpu.make_async_copy(wgu_hbm.at[:, pl.ds(pl.multiple_of(first, COLS), COLS)], wg.at[i], gu_sem.at[0, i]))
         gate_up_copies.append(pltpu.make_async_copy(wgu_hbm.at[:, pl.ds(pl.multiple_of(ffn + first, COLS), COLS)], wu.at[i], gu_sem.at[1, i]))
     barrier = pltpu.get_barrier_semaphore()
-    for step in range(1, 4):
-        pl.semaphore_signal(barrier, inc=1, device_id={'sp': lax.rem(sp + step, 4)}, device_id_type=MESH)
+    pl.semaphore_signal(barrier, inc=1, device_id={'sp': partner}, device_id_type=MESH)
     pl.semaphore_signal(barrier, inc=1, device_id={'tp': 1 - tp}, device_id_type=MESH)
-    for copy in side + out_copies[0] + out_copies[1]:
-        copy.start()
-    pl.semaphore_wait(barrier, 4)
+    for copy in side + out_copies[0] + out_copies[1] + gate_up_copies:
+        copy.start()
 
     sent = []
 
@@ -285,17 +315,8 @@
         sent.append(copy)
         return copy
 
-    first_copies = []
-    for step in (2, 1, 3):
-        peer = lax.rem(sp + step, 4)
-        first_copies.append(send(om_ref.at[lax.rem(peer, 2)], obuf.at[sp], o_send.at[step - 1], o_recv.at[step - 1], {'sp': peer}))
-    obuf[sp] = om_ref[core]
-    for copy in gate_up_copies:
-        copy.start()
-    for copy in first_copies:
-        copy.wait_recv()
-    for copy in down_copies[0] + down_copies[1]:
-        copy.start()
+    for source, ref in ((sp, own_ref), (partner, in1_ref), (lax.rem(sp + 2, 4), in2_ref), (lax.rem(partner + 2, 4), in3_ref)):
+        obuf[source] = ref[...]
 
     heads = half_width // dim
     stats = [obuf[s, :, half_width:] for s in range(4)]
@@ -334,6 +355,9 @@
         for copy in third:
             copy.wait_recv()
 
+    for copy in down_copies[0] + down_copies[1]:
+        copy.start()
+    pl.semaphore_wait(barrier, 2)
     o_copy = send(o_snd, o_got, p_send, p_recv, {'sp': partner})
     for j in range(n_half):
         acc[j] = product(o_cat[...], wo.at[0], out_copies[0], j)
@@ -371,7 +395,7 @@
         copy.wait_send()
 
 
-def layer_tail(om, hidden, norm_mlp, w_out, w_gate_up, w_down, dim):
+def layer_tail(parts, hidden, norm_mlp, w_out, w_gate_up, w_down, dim):
     rows, model = hidden.shape
     half_width, units = w_out.shape[0] // 2, w_down.shape[0] // 2
     n_wd, n_gu = model // COLS, units // COLS
@@ -383,7 +407,7 @@
     out = pl.pallas_call(
         functools.partial(tail_kernel, dim),
         out_shape=pltpu.VMEM((rows, model), f32),
-        in_specs=[vmem, hbm, hbm, hbm, hbm, hbm],
+        in_specs=[vmem] * 4 + [hbm] * 5,
         out_specs=vmem,
         scratch_shapes=[
             pltpu.VMEM((rows, model), bf16),
@@ -406,7 +430,6 @@
             pltpu.VMEM((n_gu, rows, COLS), f32),
             pltpu.VMEM((n_wd, rows, COLS), f32),
             dma((2,)), dma((2, n_half)), dma((2, n_half)), dma((2, n_gu)),
-            dma((3,)), dma((3,)),
             dma, dma,
             dma((n_gu,)), dma((n_gu,)),
             dma((2, n_half)), dma((2, n_half)),
@@ -414,7 +437,7 @@
         ],
         compiler_params=pltpu.CompilerParams(collective_id=0, has_side_effects=True, vmem_limit_bytes=54 << 20),
         name="tail",
-    )(pltpu.with_memory_space_constraint(om, pltpu.VMEM), *(pltpu.with_memory_space_constraint(x, pltpu.HBM) for x in (hidden, norm_mlp[None, :])), w_out, w_gate_up, w_down)
+    )(*(pltpu.with_memory_space_constraint(x, pltpu.VMEM) for x in parts), *(pltpu.with_memory_space_constraint(x, pltpu.HBM) for x in (hidden, norm_mlp[None, :])), w_out, w_gate_up, w_down)
     return out.astype(bf16)
 
 
@@ -425,8 +448,11 @@
         num_rows, block_len, kv_local, head_dim = k_cache.shape
         k_t, v_t = k_cache.transpose(0, 2, 3, 1), v_cache.transpose(0, 2, 3, 1)
         q_rows, new_t, k_ring, v_ring = project(positions, hidden, norm_attn, w_qkv, k_t, v_t)
-        k_upd, v_upd, om = attend(positions, q_rows, new_t, k_ring, v_ring, k_t, v_t)
-        result = layer_tail(om, hidden, norm_mlp, w_out, w_gate_up, w_down, head_dim)
+        k_upd, v_upd, own, other, k_ring, v_ring = attend(positions, q_rows, new_t, k_ring, v_ring, k_t, v_t)
+        swap = lambda value, mask: lax.ppermute(value, 'sp', [(i, i ^ mask) for i in range(4)])
+        parts = (own, swap(other, 1), swap(own, 2), swap(other, 3))
+        k_upd, v_upd = write_rest(k_ring, v_ring, k_upd, v_upd)
+        result = layer_tail(parts, hidden, norm_mlp, w_out, w_gate_up, w_down, head_dim)
         return result, k_upd.transpose(0, 3, 1, 2), v_upd.transpose(0, 3, 1, 2)
 
     return jax.shard_map(local_step, mesh=mesh, in_specs=(P('dp', None), P('dp'), P(None), P(None), P(None, 'tp'), P('tp', None), P(None, 'tp'), P('tp', None), cache_spec, cache_spec), out_specs=(P('dp', None), cache_spec, cache_spec), check_vma=False)

time: 78.4 us -> 86.4 us (1.10)
  starting transfers between devices: 0 us -> 4.1 us
  Pallas kernels: 76.8 us -> 80.8 us
    pallas_call x0 -> x1, Pallas kernels: none -> 6.57 us  [write_rest(): pl.pallas_call(write_kernel, out_shape=(jax.ShapeDtypeStruct(k_upd.shape,...]
    pallas_call x1, Pallas kernels: 38.9 us -> 33.5 us  [attend(): pl.pallas_call(attend_kernel, out_shape=(jax.ShapeDtypeStruct(k_t.shape,...]
    ppermute x0 -> x3, starting transfers between devices: none -> 4.1 us  [local_step(): lax.ppermute(value, 'sp', [(i, i ^ mask) for i in range(4)])]
    pallas_call x1, Pallas kernels: 24.9 us -> 27.7 us  [layer_tail(): pl.pallas_call(functools.partial(tail_kernel, dim), out_shape=pltpu.VMEM(...]
  transfers between devices with their start and end apart: 0 -> 3, of which waited for: 0 -> 0; matrix products, arithmetic and copies ran while one was open for 0% -> 0% of each run, Pallas kernels for 0% -> 8%
where the time goes in v9:
time: 86.4 us; the launch traced here: 86.3 us
  Pallas kernels  80.8 us (94%)
  starting transfers between devices  4.1 us (5%)
    pallas_call x1, Pallas kernels, attend(): pl.pallas_call(attend_kernel, out_shape=(jax.ShapeDtypeStruct(k_t.shape,...  33.5 us
    pallas_call x1, Pallas kernels, layer_tail(): pl.pallas_call(functools.partial(tail_kernel, dim), out_shape=pltpu.VMEM(...  27.7 us
    pallas_call x1, Pallas kernels, project(): pl.pallas_call(functools.partial(project_kernel, dim), out_shape=(pltpu.V...  13 us
    pallas_call x1, Pallas kernels, write_rest(): pl.pallas_call(write_kernel, out_shape=(jax.ShapeDtypeStruct(k_upd.shape,...  6.57 us
    ppermute x3, starting transfers between devices, local_step(): lax.ppermute(value, 'sp', [(i, i ^ mask) for i in range(4)])  4.1 us
  transfers between devices with their start and end apart: 3, of which 0 were waited for; matrix products, arithmetic and copies ran while one was open for 0% of the time, Pallas kernels for 8%

profile of v9, /device:TPU:0, one launch (start us, length us, event | category | flops | bytes accessed | tf_op | source)
XLA Modules:
  0.0 86.3 jit_solution(7752934503474101570)
XLA Ops:
  0.6 13.0 %project.1 = (f32[4,16,384]{2,1,0:T(8,128)S(1)}, f32[2,1536,128]{2,1,0:T(8,128)S(1)}, bf16[8,16,96,768]{3,2,1,0:T(8,128)(2,1)S(1)}, bf16[8,16,96,768]{3,2,1,0:T(8,128)(2,1)S(1)}) custom-call(s32[16]{0:T(128)} %pos_hbm.3, bf16[16,3072]{1,0:T(8,128)(2,1)} %hid_hbm.3, f32[1,3072]{1,0:T(1,128)} %bitcast.12, bf16[3072,4608]{1,0:T(8,128)(2,1)} %w_hbm.1, ...), custom_call_target="tpu_custom_call" | custom-call | tf_op jit(solution)/shard_map/project/pallas_call | solution.py:107
  13.7 33.5 %attend.1 = (bf16[16,16,96,768]{3,2,1,0:T(8,128)(2,1)}, bf16[16,16,96,768]{3,2,1,0:T(8,128)(2,1)}, f32[16,896]{1,0:T(8,128)S(1)}, f32[16,896]{1,0:T(8,128)S(1)},...) custom-call(s32[16]{0:T(128)} %pos_hbm.3, ...), custom_call_target="tpu_custom_call", output_to_operand_aliasing={{4}: (3, {}), {5}: (4, {})} | custom-call | tf_op jit(solution)/shard_map/attend/pallas_call | solution.py:232
  47.2 1.2 %collective-permute-start = (f32[16,896]{1,0:T(8,128)S(1)}, f32[16,896]{1,0:T(8,128)S(1)}, u32[]{:S(2)}, u32[]{:S(2)}) collective-permute-start(f32[16,896]{1,0:T(8,128)S(1)} %get-tuple-element.20), channel_id=1, source_target_pairs={{0,1},{1,0},{2,3},{3,2},{4,5},{5,4},{6,7},{7,6}} | collective-permute-start | bytes 172040 | tf_op jit(solution)/shard_map/ppermute | solution.py:452
  48.4 2.5 %collective-permute-start.2 = (f32[16,896]{1,0:T(8,128)S(1)}, f32[16,896]{1,0:T(8,128)S(1)}, u32[]{:S(2)}, u32[]{:S(2)}) collective-permute-start(f32[16,896]{1,0:T(8,128)S(1)} %get-tuple-element.20), channel_id=1, source_target_pairs={{0,3},{1,2},{2,1},{3,0},{4,7},{5,6},{6,5},{7,4}} | collective-permute-start | bytes 172040 | tf_op jit(solution)/shard_map/ppermute | solution.py:452
  50.9 0.4 collective-permute-start.1
  51.3 6.6 %write_rest.1 = (bf16[16,16,96,768]{3,2,1,0:T(8,128)(2,1)}, bf16[16,16,96,768]{3,2,1,0:T(8,128)(2,1)}) custom-call(bf16[8,16,96,768]{3,2,1,0:T(8,128)(2,1)S(1)} %get-tuple-element.21.k_ring, bf16[8,16,96,768]{3,2,1,0:T(8,128)(2,1)S(1)} %get-tuple-element.22.v_ring, ...), custom_call_target="tpu_custom_call", output_to_operand_aliasing={{0}: (2, {}), {1}: (3, {})} | custom-call | flops 10000000000 | bytes 19922944 | tf_op jit(solution)/shard_map/write_rest/pallas_call | solution.py:262
  57.8 0.0 collective-permute-done.in1_ref
  57.9 0.0 collective-permute-done.1.in2_ref
  57.9 0.0 collective-permute-done.2.in3_ref
  57.9 27.7 %tail.1 = f32[16,3072]{1,0:T(8,128)S(1)} custom-call(f32[16,896]{1,0:T(8,128)S(1)} %get-tuple-element.19.own_ref, f32[16,896]{1,0:T(8,128)S(1)} %collective-permute-done.in1_ref, f32[16,896]{1,0:T(8,128)S(1)} %collective-permute-done.1.in2_ref, f32[16,896]{1,0:T(8,128)S(1)} %collective-permute-done.2.in3_ref, bf16[16,3072]{1,0:T(8,128)(2,1)} %hid_hbm.3, ...), custom_call_target="tpu_custom_call" | custom-call | tf_op jit(solution)/shard_map/tail/pallas_call | solution.py:407
  85.6 0.7 convert_element_type.3
Async XLA Ops:
  47.2 10.7 %collective-permute-start = (f32[16,896]{1,0:T(8,128)S(1)}, f32[16,896]{1,0:T(8,128)S(1)}, u32[]{:S(2)}, u32[]{:S(2)}) collective-permute-start(f32[16,896]{1,0:T(8,128)S(1)} %get-tuple-element.20), channel_id=1, source_target_pairs={{0,1},{1,0},{2,3},{3,2},{4,5},{5,4},{6,7},{7,6}} | collective-permute-start | bytes 172040 | tf_op jit(solution)/shard_map/ppermute | solution.py:452
  48.4 9.5 %collective-permute-start.2 = (f32[16,896]{1,0:T(8,128)S(1)}, f32[16,896]{1,0:T(8,128)S(1)}, u32[]{:S(2)}, u32[]{:S(2)}) collective-permute-start(f32[16,896]{1,0:T(8,128)S(1)} %get-tuple-element.20), channel_id=1, source_target_pairs={{0,3},{1,2},{2,1},{3,0},{4,7},{5,6},{6,5},{7,4}} | collective-permute-start | bytes 172040 | tf_op jit(solution)/shard_map/ppermute | solution.py:452
  50.9 7.0 %collective-permute-start.1 = (f32[16,896]{1,0:T(8,128)S(1)}, f32[16,896]{1,0:T(8,128)S(1)}, u32[]{:S(2)}, u32[]{:S(2)}) collective-permute-start(f32[16,896]{1,0:T(8,128)S(1)} %get-tuple-element.19.own_ref), channel_id=1, source_target_pairs={{0,2},{1,3},{2,0},{3,1},{4,6},{5,7},{6,4},{7,5}} | collective-permute-start | bytes 172040 | tf_op jit(solution)/shard_map/ppermute | solution.py:452

commit v10 on v7

--- a/solution.py
+++ b/solution.py
@@ -294,8 +294,6 @@
         copy.start()
     for copy in first_copies:
         copy.wait_recv()
-    for copy in down_copies[0] + down_copies[1]:
-        copy.start()
 
     heads = half_width // dim
     stats = [obuf[s, :, half_width:] for s in range(4)]
@@ -329,6 +327,9 @@
         third = []
         for j in range(n_half):
             second[j].wait_recv()
+            if stage == 0 and j == 0:
+                for copy in down_copies[0] + down_copies[1]:
+                    copy.start()
             dst[core * n_half + j] = base_of(j) + (ysnd[stage, j] + ygot[stage, j])
             third.append(send(dst.at[core * n_half + j], dst.at[core * n_half + j], g_send.at[stage, j], g_recv.at[stage, j], {'sp': partner}))
         for copy in third:

time: 78.4 us -> 78.3 us (level)
  no operation moved by 1% of the time
where the time goes in v10:
time: 78.3 us; the launch traced here: 77.6 us
  Pallas kernels  76.3 us (97%)
    pallas_call x1, Pallas kernels, attend(): pl.pallas_call(attend_kernel, out_shape=(jax.ShapeDtypeStruct(k_t.shape,...  38.9 us
    pallas_call x1, Pallas kernels, layer_tail(): pl.pallas_call(functools.partial(tail_kernel, dim), out_shape=pltpu.VMEM(...  24.3 us
    pallas_call x1, Pallas kernels, project(): pl.pallas_call(functools.partial(project_kernel, dim), out_shape=(pltpu.V...  13 us

profile of v10, /device:TPU:0, one launch (start us, length us, event | category | flops | bytes accessed | tf_op | source)
XLA Modules:
  0.0 77.6 jit_solution(17593642810903545254)
XLA Ops:
  0.6 13.0 %project.1 = (f32[4,16,384]{2,1,0:T(8,128)S(1)}, f32[2,1536,128]{2,1,0:T(8,128)S(1)}, bf16[8,16,96,768]{3,2,1,0:T(8,128)(2,1)S(1)}, bf16[8,16,96,768]{3,2,1,0:T(8,128)(2,1)S(1)}) custom-call(s32[16]{0:T(128)} %pos_hbm.3, bf16[16,3072]{1,0:T(8,128)(2,1)} %hid_hbm.3, f32[1,3072]{1,0:T(1,128)} %bitcast.10, bf16[3072,4608]{1,0:T(8,128)(2,1)} %w_hbm.1, ...), custom_call_target="tpu_custom_call" | custom-call | tf_op jit(solution)/shard_map/project/pallas_call | solution.py:106
  13.7 38.9 %attend.1 = (bf16[16,16,96,768]{3,2,1,0:T(8,128)(2,1)}, bf16[16,16,96,768]{3,2,1,0:T(8,128)(2,1)}, f32[2,16,896]{2,1,0:T(8,128)S(1)}, bf16[8,16,96,768]{3,2,1,0:T(8,128)(2,1)S(1)}, bf16[8,16,96,768]{3,2,1,0:T(8,128)(2,1)S(1)}) custom-call(s32[16]{0:T(128)} %pos_hbm.3, ...), custom_call_target="tpu_custom_call", output_to_operand_aliasing={{3}: (3, {}), {4}: (4, {})} | custom-call | tf_op jit(solution)/shard_map/attend/pallas_call | solution.py:227
  52.6 24.3 %tail.1 = f32[16,3072]{1,0:T(8,128)S(1)} custom-call(f32[2,16,896]{2,1,0:T(8,128)S(1)} %get-tuple-element.14.om_ref, bf16[16,3072]{1,0:T(8,128)(2,1)} %hid_hbm.3, f32[1,3072]{1,0:T(1,128)} %bitcast.11, bf16[1536,3072]{1,0:T(8,128)(2,1)} %wo_hbm.1, bf16[3072,8192]{1,0:T(8,128)(2,1)} %wgu_hbm.1, bf16[4096,3072]{1,0:T(8,128)(2,1)} %wd_hbm.1), custom_call_target="tpu_custom_call" | custom-call | tf_op jit(solution)/shard_map/tail/pallas_call | solution.py:384
  76.9 0.7 convert_element_type.3
